TPU v7x, 32 devices: a whole 2x2x4 slice. The times are simulated.
32 devices in a mesh: gx: 4 (over y, core), gy: 8 (over z, x).
Axes of the slice: x: 2, y: 2, z: 4, core: 2. Of those that a mesh axis runs over, the one named last changes fastest.
Arguments:
- disp: float32 [3, 32, 128, 128], P(None, 'gx', 'gy'), may hold values from -3 to 3
- vel: float32 [3, 32, 128, 128], P(None, 'gx', 'gy'), may hold values from -30 to 30
- load: float32 [3, 32, 128, 128], P(None, 'gx', 'gy'), may hold values from -96 to 96
- flags: int32 [32, 128, 128], P('gx', 'gy'), may hold values 0 or 1
- mask_bits: int32 [4, 32, 128, 128], P(None, 'gx', 'gy'), may hold values from 0 to 2147483647, as said below
Outputs:
- disp_out: float32 [3, 32, 128, 128], P(None, 'gx', 'gy')
- vel_out: float32 [3, 32, 128, 128], P(None, 'gx', 'gy')
Inputs may be any that keep to these rules, and one draw needn't show every extreme that they name: `mask_bits`: bit b (0 to 30) of word w marks the cell's bond to neighbour number 31 w + b as broken; bit 31, and bits of numbers 122 and above, are zero.
All inputs are finite; a program needn't handle non-finite values. No bound on the sum of `flags` on one device may be relied on, other than what follows from the above.
Results may differ from a plain program's by a relative error of at most 0.0001.
Values sent between devices are 32-bit elements; how exact they have to be, the bound alone decides.
No kernel may reach another device: no remote copies, remote signals or barrier semaphores. Data moves between devices by JAX's collectives and lax.ppermute only.
A program may use at most 128 MiB of HBM per device.

v0:
```python
import math

import jax
import jax.numpy as jnp
from jax import lax
from jax.sharding import PartitionSpec as P

ITERS = 8


fictive_mass = 64.0
epsilon = 1e-06


def extended(cells, sides, width):
    for axis, dim in sides:
        count = lax.axis_size(axis)
        ends = count - 1
        head = lax.slice_in_dim(cells, 0, width, axis=dim)
        tail = lax.slice_in_dim(cells, cells.shape[dim] - width, cells.shape[dim], axis=dim)
        cells = jnp.concatenate(
            [
                lax.ppermute(tail, axis, [(i, (i + 1) % count) for i in range(ends)]),
                cells,
                lax.ppermute(head, axis, [((i + 1) % count, i) for i in range(ends)]),
            ],
            axis=dim,
        )
    return cells


def neighbour_table():
    table = []
    for across in range(-3, 4):
        for along in range(-3, 4):
            for upward in range(-3, 4):
                length = across * across + along * along + upward * upward
                if 0 < length <= 9:
                    table.append((across, along, upward))
    return table


def bond_forces(field_pad, words, words_pad, exist_pad):
    rows = words.shape[1]
    cols = words.shape[2]
    depth = words.shape[3]
    centre = field_pad[:, 3 : 3 + rows, 3 : 3 + cols, 3 : 3 + depth]
    totals = [jnp.zeros((rows, cols, depth), jnp.float32) for index in range(3)]
    for number, offset in enumerate(neighbour_table()):
        across, along, upward = offset
        word, bit = divmod(number, 31)
        mirror_word, mirror_bit = divmod(121 - number, 31)
        window = (
            slice(3 + across, 3 + across + rows),
            slice(3 + along, 3 + along + cols),
            slice(3 + upward, 3 + upward + depth),
        )
        other = field_pad[(slice(None),) + window]
        own_flag = words[word] >> bit & 1
        far_flag = words_pad[mirror_word][window] >> mirror_bit & 1
        intact = (own_flag | far_flag == 0) & (exist_pad[window] > 0)
        length = float(across * across + along * along + upward * upward)
        weight = 1.0 / (length * math.sqrt(length))
        stretch = (
            float(across) * (other[0] - centre[0])
            + float(along) * (other[1] - centre[1])
            + float(upward) * (other[2] - centre[2])
        )
        scaled = jnp.where(intact, stretch * weight, jnp.float32(0.0))
        totals[0] = totals[0] + float(across) * scaled
        totals[1] = totals[1] + float(along) * scaled
        totals[2] = totals[2] + float(upward) * scaled
    return jnp.stack(totals)


def depth_pad(field):
    return jnp.pad(field, ((0, 0), (0, 0), (0, 0), (3, 3)))


def on_device(disp, vel, load, flags, mask_bits):
    rows = disp.shape[1]
    cols = disp.shape[2]
    depth = disp.shape[3]
    size_x = lax.axis_size("gx")
    size_y = lax.axis_size("gy")
    count = 3.0 * rows * size_x * cols * size_y * depth
    words_rim = extended(mask_bits, (("gx", 1), ("gy", 2)), 3)
    words_pad = depth_pad(words_rim)
    places_x = lax.axis_index("gx") * rows - 3 + jnp.arange(rows + 6, dtype=jnp.int32)
    places_y = lax.axis_index("gy") * cols - 3 + jnp.arange(cols + 6, dtype=jnp.int32)
    places_z = jnp.arange(depth + 6, dtype=jnp.int32)
    inside_x = (places_x >= 0) & (places_x < rows * size_x)
    inside_y = (places_y >= 0) & (places_y < cols * size_y)
    inside_z = (places_z >= 3) & (places_z < depth + 3)
    exist_pad = (
        inside_x[:, None, None] & inside_y[None, :, None] & inside_z[None, None, :]
    ).astype(jnp.int32)
    applied = flags.astype(jnp.float32)[None] * load

    def internal(field):
        field_rim = extended(field, (("gx", 1), ("gy", 2)), 3)
        return bond_forces(depth_pad(field_rim), mask_bits, words_pad, exist_pad)

    previous = internal(disp - vel)
    field = disp
    speed = vel
    for step in range(ITERS):
        current = internal(field)
        total = current + applied
        kinetic, rayleigh = lax.psum(
            (jnp.sum(speed * speed), jnp.sum(speed * (previous - current))), ("gx", "gy")
        )
        damping = 2.0 * jnp.sqrt(rayleigh / count / (fictive_mass * (kinetic / count + epsilon)))
        alpha = (2.0 - damping) / (2.0 + damping)
        beta = 2.0 / (fictive_mass * (2.0 + damping))
        alpha, beta = (alpha, beta)
        speed = alpha * speed + beta * total
        field = field + speed
        previous = current
    return (field, speed)


def solution(mesh):
    placed = (
        P(None, "gx", "gy", None),
        P(None, "gx", "gy", None),
        P(None, "gx", "gy", None),
        P("gx", "gy", None),
        P(None, "gx", "gy", None),
    )
    return jax.shard_map(
        on_device,
        mesh=mesh,
        in_specs=placed,
        out_specs=(P(None, "gx", "gy", None), P(None, "gx", "gy", None)),
        check_vma=False,
    )
```

profile of v0, /device:TPU:0, one launch (start us, length us, event | category | flops | bytes accessed | tf_op | source)
XLA Modules:
  0.0 608.1 jit_solution(17983634218505052696)
XLA Ops:
  5.0 4.5 collective-permute-start
  13.9 4.3 collective-permute-start.4
  19.6 4.6 collective-permute-start.10
  25.6 4.9 collective-permute-start.2
  31.1 4.8 collective-permute-start.6
  44.0 8.3 %add_bitcast_fusion.23 = (f32[1,8,16,128]{3,2,1,0:T(8,128)S(1)}, f32[8,16,128]{2,1,0:T(8,128)S(1)}, pred[8,16,128]{2,1,0:T(8,128)(4,1)S(1)}, f32[8,16,128]{2,1,0...) fusion(f32[8,16,128]{2,1,0:T(8,128)S(1)} %get-tuple-element.129, ...), kind=kLoop, calls=%fused_computation.12535 | loop fusion | flops 22806528 | bytes 33044480 | tf_op jit(solution)/shard_map/stack | solution.py:73
  54.4 7.3 %add_bitcast_fusion.26 = (f32[1,8,16,128]{3,2,1,0:T(8,128)S(1)}, f32[8,16,128]{2,1,0:T(8,128)S(1)}, f32[8,16,128]{2,1,0:T(8,128)S(1)}, f32[8,16,128]{2,1,0:T(8,1...) fusion(f32[8,16,128]{2,1,0:T(8,128)S(1)} %get-tuple-element.111, ...), kind=kLoop, calls=%fused_computation.12538 | loop fusion | flops 20709376 | bytes 31277056 | tf_op jit(solution)/shard_map/stack | solution.py:73
  64.1 42.3 %all-reduce.17 = (f32[]{:T(128)}, f32[]{:T(128)}) all-reduce(f32[]{:T(128)} %get-tuple-element.17, f32[]{:T(128)} %get-tuple-element.16), channel_id=1, replica_groups=mesh['gx'=4,'gy'=8] {'gx','gy'}, use_global_device_ids=true, to_apply=%region_1.2 | all-reduce | flops 2 | bytes 16 | tf_op jit(solution)/shard_map/psum | solution.py:110
  113.2 4.2 collective-permute-start.14
  125.0 7.3 %add_bitcast_fusion.20 = (f32[1,8,16,128]{3,2,1,0:T(8,128)S(1)}, f32[8,16,128]{2,1,0:T(8,128)S(1)}, f32[8,16,128]{2,1,0:T(8,128)S(1)}, f32[8,16,128]{2,1,0:T(8,1...) fusion(f32[8,16,128]{2,1,0:T(8,128)S(1)} %get-tuple-element.127, ...), kind=kLoop, calls=%fused_computation.12532 | loop fusion | flops 20709376 | bytes 31277056 | tf_op jit(solution)/shard_map/stack | solution.py:73
  134.7 42.6 %all-reduce.16 = (f32[]{:T(128)}, f32[]{:T(128)}) all-reduce(f32[]{:T(128)} %get-tuple-element.15, f32[]{:T(128)} %get-tuple-element.14), channel_id=1, replica_groups=mesh['gx'=4,'gy'=8] {'gx','gy'}, use_global_device_ids=true, to_apply=%region_5.6 | all-reduce | flops 2 | bytes 16 | tf_op jit(solution)/shard_map/psum | solution.py:110
  185.0 4.2 collective-permute-start.18
  191.6 4.1 collective-permute-done.19
  196.8 7.3 %add_bitcast_fusion.17 = (f32[1,8,16,128]{3,2,1,0:T(8,128)S(1)}, f32[8,16,128]{2,1,0:T(8,128)S(1)}, f32[8,16,128]{2,1,0:T(8,128)S(1)}, f32[8,16,128]{2,1,0:T(8,1...) fusion(f32[8,16,128]{2,1,0:T(8,128)S(1)} %get-tuple-element.126, ...), kind=kLoop, calls=%fused_computation.12529 | loop fusion | flops 20709376 | bytes 31277056 | tf_op jit(solution)/shard_map/stack | solution.py:73
  206.4 42.7 %all-reduce.15 = (f32[]{:T(128)}, f32[]{:T(128)}) all-reduce(f32[]{:T(128)} %get-tuple-element.13, f32[]{:T(128)} %get-tuple-element.12), channel_id=1, replica_groups=mesh['gx'=4,'gy'=8] {'gx','gy'}, use_global_device_ids=true, to_apply=%region_9.10 | all-reduce | flops 2 | bytes 16 | tf_op jit(solution)/shard_map/psum | solution.py:110
  256.8 4.2 collective-permute-start.22
  268.6 7.3 %add_bitcast_fusion.14 = (f32[1,8,16,128]{3,2,1,0:T(8,128)S(1)}, f32[8,16,128]{2,1,0:T(8,128)S(1)}, f32[8,16,128]{2,1,0:T(8,128)S(1)}, f32[8,16,128]{2,1,0:T(8,1...) fusion(f32[8,16,128]{2,1,0:T(8,128)S(1)} %get-tuple-element.125, ...), kind=kLoop, calls=%fused_computation.12526 | loop fusion | flops 20709376 | bytes 31277056 | tf_op jit(solution)/shard_map/stack | solution.py:73
  278.2 42.6 %all-reduce.14 = (f32[]{:T(128)}, f32[]{:T(128)}) all-reduce(f32[]{:T(128)} %get-tuple-element.11, f32[]{:T(128)} %get-tuple-element.10), channel_id=1, replica_groups=mesh['gx'=4,'gy'=8] {'gx','gy'}, use_global_device_ids=true, to_apply=%region_13.14 | all-reduce | flops 2 | bytes 16 | tf_op jit(solution)/shard_map/psum | solution.py:110
  327.7 4.2 collective-permute-start.26
  334.3 4.1 collective-permute-done.27
  339.5 7.3 %add_bitcast_fusion.11 = (f32[1,8,16,128]{3,2,1,0:T(8,128)S(1)}, f32[8,16,128]{2,1,0:T(8,128)S(1)}, f32[8,16,128]{2,1,0:T(8,128)S(1)}, f32[8,16,128]{2,1,0:T(8,1...) fusion(f32[8,16,128]{2,1,0:T(8,128)S(1)} %get-tuple-element.124, ...), kind=kLoop, calls=%fused_computation.12523 | loop fusion | flops 20709376 | bytes 31277056 | tf_op jit(solution)/shard_map/stack | solution.py:73
  349.2 42.6 %all-reduce.13 = (f32[]{:T(128)}, f32[]{:T(128)}) all-reduce(f32[]{:T(128)} %get-tuple-element.9, f32[]{:T(128)} %get-tuple-element.8), channel_id=1, replica_groups=mesh['gx'=4,'gy'=8] {'gx','gy'}, use_global_device_ids=true, to_apply=%region_17.18 | all-reduce | flops 2 | bytes 16 | tf_op jit(solution)/shard_map/psum | solution.py:110
  399.5 4.2 collective-permute-start.30
  406.1 4.1 collective-permute-done.31
  411.3 7.3 %add_bitcast_fusion.8 = (f32[1,8,16,128]{3,2,1,0:T(8,128)S(1)}, f32[8,16,128]{2,1,0:T(8,128)S(1)}, f32[8,16,128]{2,1,0:T(8,128)S(1)}, f32[8,16,128]{2,1,0:T(8,12...) fusion(f32[8,16,128]{2,1,0:T(8,128)S(1)} %get-tuple-element.123, ...), kind=kLoop, calls=%fused_computation.12520 | loop fusion | flops 20709376 | bytes 31277056 | tf_op jit(solution)/shard_map/stack | solution.py:73
  420.9 42.7 %all-reduce.12 = (f32[]{:T(128)}, f32[]{:T(128)}) all-reduce(f32[]{:T(128)} %get-tuple-element.7, f32[]{:T(128)} %get-tuple-element.6), channel_id=1, replica_groups=mesh['gx'=4,'gy'=8] {'gx','gy'}, use_global_device_ids=true, to_apply=%region_21.22 | all-reduce | flops 2 | bytes 16 | tf_op jit(solution)/shard_map/psum | solution.py:110
  470.4 4.2 collective-permute-start.34
  482.2 7.3 %add_bitcast_fusion.5 = (f32[1,8,16,128]{3,2,1,0:T(8,128)S(1)}, f32[8,16,128]{2,1,0:T(8,128)S(1)}, f32[8,16,128]{2,1,0:T(8,128)S(1)}, f32[8,16,128]{2,1,0:T(8,12...) fusion(f32[8,16,128]{2,1,0:T(8,128)S(1)} %get-tuple-element.122, ...), kind=kLoop, calls=%fused_computation.12517 | loop fusion | flops 20709376 | bytes 31277056 | tf_op jit(solution)/shard_map/stack | solution.py:73
  491.8 42.6 %all-reduce.11 = (f32[]{:T(128)}, f32[]{:T(128)}) all-reduce(f32[]{:T(128)} %get-tuple-element.5, f32[]{:T(128)} %get-tuple-element.4), channel_id=1, replica_groups=mesh['gx'=4,'gy'=8] {'gx','gy'}, use_global_device_ids=true, to_apply=%region_25.26 | all-reduce | flops 2 | bytes 16 | tf_op jit(solution)/shard_map/psum | solution.py:110
  541.3 4.2 collective-permute-start.38
  553.0 7.3 %add_bitcast_fusion.2 = (f32[1,8,16,128]{3,2,1,0:T(8,128)S(1)}, f32[8,16,128]{2,1,0:T(8,128)S(1)}, f32[8,16,128]{2,1,0:T(8,128)S(1)}, f32[8,16,128]{2,1,0:T(8,12...) fusion(f32[8,16,128]{2,1,0:T(8,128)S(1)} %get-tuple-element.121, ...), kind=kLoop, calls=%fused_computation.12514 | loop fusion | flops 20709376 | bytes 31277056 | tf_op jit(solution)/shard_map/stack | solution.py:73
  562.7 42.6 %all-reduce.10 = (f32[]{:T(128)}, f32[]{:T(128)}) all-reduce(f32[]{:T(128)} %get-tuple-element.3, f32[]{:T(128)} %get-tuple-element.2), channel_id=1, replica_groups=mesh['gx'=4,'gy'=8] {'gx','gy'}, use_global_device_ids=true, to_apply=%region_29.30 | all-reduce | flops 2 | bytes 16 | tf_op jit(solution)/shard_map/psum | solution.py:110
  (249 shorter events, 121.7 us)
Async XLA Ops:
  1.7 10.8 %collective-permute-start.8 = (f32[3,3,16,128]{3,2,1,0:T(8,128)S(1)}, f32[3,3,16,128]{3,2,1,0:T(8,128)S(1)}, u32[]{:S(2)}, u32[]{:S(2)}) collective-permute-start(f32[3,3,16,128]{3,2,1,0:T(8,128)S(1)} %get-tuple-element.1356), channel_id=1, source_target_pairs={{0,8},{8,16},{16,24},{1,9},{9,17},{17,25},{2,10},{10,18},{18,26},{... | collective-permute-start | bytes 221192 | tf_op jit(solution)/shard_map/ppermute | solution.py:23
  5.0 14.5 %collective-permute-start = (s32[4,3,16,128]{3,2,1,0:T(8,128)S(1)}, s32[4,3,16,128]{3,2,1,0:T(8,128)S(1)}, u32[]{:S(2)}, u32[]{:S(2)}) collective-permute-start(s32[4,3,16,128]{3,2,1,0:T(8,128)S(1)} %get-tuple-element.1336), channel_id=1, source_target_pairs={{0,8},{8,16},{16,24},{1,9},{9,17},{17,25},{2,10},{10,18},{18,26},{... | collective-permute-start | bytes 294920 | tf_op jit(solution)/shard_map/ppermute | solution.py:23
  9.6 14.6 %collective-permute-start.1 = (s32[4,3,16,128]{3,2,1,0:T(8,128)S(1)}, s32[4,3,16,128]{3,2,1,0:T(8,128)S(1)}, u32[]{:S(2)}, u32[]{:S(2)}) collective-permute-start(s32[4,3,16,128]{3,2,1,0:T(8,128)S(1)} %get-tuple-element.1335), channel_id=1, source_target_pairs={{8,0},{16,8},{24,16},{9,1},{17,9},{25,17},{10,2},{18,10},{26,18},{... | collective-permute-start | bytes 294920 | tf_op jit(solution)/shard_map/ppermute | solution.py:25
  10.9 7.3 %collective-permute-start.9 = (f32[3,3,16,128]{3,2,1,0:T(8,128)S(1)}, f32[3,3,16,128]{3,2,1,0:T(8,128)S(1)}, u32[]{:S(2)}, u32[]{:S(2)}) collective-permute-start(f32[3,3,16,128]{3,2,1,0:T(8,128)S(1)} %get-tuple-element.1355), channel_id=1, source_target_pairs={{8,0},{16,8},{24,16},{9,1},{17,9},{25,17},{10,2},{18,10},{26,18},{... | collective-permute-start | bytes 221192 | tf_op jit(solution)/shard_map/ppermute | solution.py:25
  12.6 18.5 %collective-permute-start.5 = (f32[3,3,16,128]{3,2,1,0:T(8,128)S(1)}, f32[3,3,16,128]{3,2,1,0:T(8,128)S(1)}, u32[]{:S(2)}, u32[]{:S(2)}) collective-permute-start(f32[3,3,16,128]{3,2,1,0:T(8,128)S(1)} %get-tuple-element.1358), channel_id=1, source_target_pairs={{8,0},{16,8},{24,16},{9,1},{17,9},{25,17},{10,2},{18,10},{26,18},{... | collective-permute-start | bytes 221192 | tf_op jit(solution)/shard_map/ppermute | solution.py:25
  13.9 17.2 %collective-permute-start.4 = (f32[3,3,16,128]{3,2,1,0:T(8,128)S(1)}, f32[3,3,16,128]{3,2,1,0:T(8,128)S(1)}, u32[]{:S(2)}, u32[]{:S(2)}) collective-permute-start(f32[3,3,16,128]{3,2,1,0:T(8,128)S(1)} %get-tuple-element.1357), channel_id=1, source_target_pairs={{0,8},{8,16},{16,24},{1,9},{9,17},{17,25},{2,10},{10,18},{18,26},{... | collective-permute-start | bytes 221192 | tf_op jit(solution)/shard_map/ppermute | solution.py:23
  18.3 7.3 %collective-permute-start.11 = (f32[3,14,3,128]{3,2,1,0:T(4,128)S(1)}, f32[3,14,3,128]{3,2,1,0:T(4,128)S(1)}, u32[]{:S(2)}, u32[]{:S(2)}) collective-permute-start(f32[3,14,3,128]{3,2,1,0:T(4,128)S(1)} %get-tuple-element.1330), channel_id=1, source_target_pairs={{1,0},{2,1},{3,2},{4,3},{5,4},{6,5},{7,6},{9,8},{10,9},{11,10},{12... | collective-permute-start | bytes 193544 | tf_op jit(solution)/shard_map/ppermute | solution.py:25
  19.6 10.9 %collective-permute-start.10 = (f32[3,14,3,128]{3,2,1,0:T(4,128)S(1)}, f32[3,14,3,128]{3,2,1,0:T(4,128)S(1)}, u32[]{:S(2)}, u32[]{:S(2)}) collective-permute-start(f32[3,14,3,128]{3,2,1,0:T(4,128)S(1)} %get-tuple-element.1329), channel_id=1, source_target_pairs={{0,1},{1,2},{2,3},{3,4},{4,5},{5,6},{6,7},{8,9},{9,10},{10,11},{11... | collective-permute-start | bytes 193544 | tf_op jit(solution)/shard_map/ppermute | solution.py:23
  24.3 13.0 %collective-permute-start.3 = (s32[4,14,3,128]{3,2,1,0:T(4,128)S(1)}, s32[4,14,3,128]{3,2,1,0:T(4,128)S(1)}, u32[]{:S(2)}, u32[]{:S(2)}) collective-permute-start(s32[4,14,3,128]{3,2,1,0:T(4,128)S(1)} %get-tuple-element.1300), channel_id=1, source_target_pairs={{1,0},{2,1},{3,2},{4,3},{5,4},{6,5},{7,6},{9,8},{10,9},{11,10},{12... | collective-permute-start | bytes 258056 | tf_op jit(solution)/shard_map/ppermute | solution.py:25
  25.6 11.7 %collective-permute-start.2 = (s32[4,14,3,128]{3,2,1,0:T(4,128)S(1)}, s32[4,14,3,128]{3,2,1,0:T(4,128)S(1)}, u32[]{:S(2)}, u32[]{:S(2)}) collective-permute-start(s32[4,14,3,128]{3,2,1,0:T(4,128)S(1)} %get-tuple-element.1299), channel_id=1, source_target_pairs={{0,1},{1,2},{2,3},{3,4},{4,5},{5,6},{6,7},{8,9},{9,10},{10,11},{11... | collective-permute-start | bytes 258056 | tf_op jit(solution)/shard_map/ppermute | solution.py:23
  31.1 11.2 %collective-permute-start.6 = (f32[3,14,3,128]{3,2,1,0:T(4,128)S(1)}, f32[3,14,3,128]{3,2,1,0:T(4,128)S(1)}, u32[]{:S(2)}, u32[]{:S(2)}) collective-permute-start(f32[3,14,3,128]{3,2,1,0:T(4,128)S(1)} %get-tuple-element.1333), channel_id=1, source_target_pairs={{0,1},{1,2},{2,3},{3,4},{4,5},{5,6},{6,7},{8,9},{9,10},{10,11},{11... | collective-permute-start | bytes 193544 | tf_op jit(solution)/shard_map/ppermute | solution.py:23
  35.9 6.7 %collective-permute-start.7 = (f32[3,14,3,128]{3,2,1,0:T(4,128)S(1)}, f32[3,14,3,128]{3,2,1,0:T(4,128)S(1)}, u32[]{:S(2)}, u32[]{:S(2)}) collective-permute-start(f32[3,14,3,128]{3,2,1,0:T(4,128)S(1)} %get-tuple-element.1334), channel_id=1, source_target_pairs={{1,0},{2,1},{3,2},{4,3},{5,4},{6,5},{7,6},{9,8},{10,9},{11,10},{12... | collective-permute-start | bytes 193544 | tf_op jit(solution)/shard_map/ppermute | solution.py:25
  107.9 4.3 collective-permute-start.13
  113.2 6.6 %collective-permute-start.14 = (f32[3,14,3,128]{3,2,1,0:T(4,128)S(1)}, f32[3,14,3,128]{3,2,1,0:T(4,128)S(1)}, u32[]{:S(2)}, u32[]{:S(2)}) collective-permute-start(f32[3,14,3,128]{3,2,1,0:T(4,128)S(1)} %get-tuple-element.1327), channel_id=1, source_target_pairs={{0,1},{1,2},{2,3},{3,4},{4,5},{5,6},{6,7},{8,9},{9,10},{10,11},{11... | collective-permute-start | bytes 193544 | tf_op jit(solution)/shard_map/ppermute | solution.py:23
  117.4 6.6 %collective-permute-start.15 = (f32[3,14,3,128]{3,2,1,0:T(4,128)S(1)}, f32[3,14,3,128]{3,2,1,0:T(4,128)S(1)}, u32[]{:S(2)}, u32[]{:S(2)}) collective-permute-start(f32[3,14,3,128]{3,2,1,0:T(4,128)S(1)} %get-tuple-element.1328), channel_id=1, source_target_pairs={{1,0},{2,1},{3,2},{4,3},{5,4},{6,5},{7,6},{9,8},{10,9},{11,10},{12... | collective-permute-start | bytes 193544 | tf_op jit(solution)/shard_map/ppermute | solution.py:25
  179.7 4.3 collective-permute-start.17
  185.0 6.6 %collective-permute-start.18 = (f32[3,14,3,128]{3,2,1,0:T(4,128)S(1)}, f32[3,14,3,128]{3,2,1,0:T(4,128)S(1)}, u32[]{:S(2)}, u32[]{:S(2)}) collective-permute-start(f32[3,14,3,128]{3,2,1,0:T(4,128)S(1)} %get-tuple-element.1323), channel_id=1, source_target_pairs={{0,1},{1,2},{2,3},{3,4},{4,5},{5,6},{6,7},{8,9},{9,10},{10,11},{11... | collective-permute-start | bytes 193544 | tf_op jit(solution)/shard_map/ppermute | solution.py:23
  189.2 6.6 %collective-permute-start.19 = (f32[3,14,3,128]{3,2,1,0:T(4,128)S(1)}, f32[3,14,3,128]{3,2,1,0:T(4,128)S(1)}, u32[]{:S(2)}, u32[]{:S(2)}) collective-permute-start(f32[3,14,3,128]{3,2,1,0:T(4,128)S(1)} %get-tuple-element.1324), channel_id=1, source_target_pairs={{1,0},{2,1},{3,2},{4,3},{5,4},{6,5},{7,6},{9,8},{10,9},{11,10},{12... | collective-permute-start | bytes 193544 | tf_op jit(solution)/shard_map/ppermute | solution.py:25
  251.6 4.3 collective-permute-start.21
  256.8 6.6 %collective-permute-start.22 = (f32[3,14,3,128]{3,2,1,0:T(4,128)S(1)}, f32[3,14,3,128]{3,2,1,0:T(4,128)S(1)}, u32[]{:S(2)}, u32[]{:S(2)}) collective-permute-start(f32[3,14,3,128]{3,2,1,0:T(4,128)S(1)} %get-tuple-element.1319), channel_id=1, source_target_pairs={{0,1},{1,2},{2,3},{3,4},{4,5},{5,6},{6,7},{8,9},{9,10},{10,11},{11... | collective-permute-start | bytes 193544 | tf_op jit(solution)/shard_map/ppermute | solution.py:23
  261.0 6.6 %collective-permute-start.23 = (f32[3,14,3,128]{3,2,1,0:T(4,128)S(1)}, f32[3,14,3,128]{3,2,1,0:T(4,128)S(1)}, u32[]{:S(2)}, u32[]{:S(2)}) collective-permute-start(f32[3,14,3,128]{3,2,1,0:T(4,128)S(1)} %get-tuple-element.1320), channel_id=1, source_target_pairs={{1,0},{2,1},{3,2},{4,3},{5,4},{6,5},{7,6},{9,8},{10,9},{11,10},{12... | collective-permute-start | bytes 193544 | tf_op jit(solution)/shard_map/ppermute | solution.py:25
  322.4 4.3 collective-permute-start.25
  327.7 6.6 %collective-permute-start.26 = (f32[3,14,3,128]{3,2,1,0:T(4,128)S(1)}, f32[3,14,3,128]{3,2,1,0:T(4,128)S(1)}, u32[]{:S(2)}, u32[]{:S(2)}) collective-permute-start(f32[3,14,3,128]{3,2,1,0:T(4,128)S(1)} %get-tuple-element.1315), channel_id=1, source_target_pairs={{0,1},{1,2},{2,3},{3,4},{4,5},{5,6},{6,7},{8,9},{9,10},{10,11},{11... | collective-permute-start | bytes 193544 | tf_op jit(solution)/shard_map/ppermute | solution.py:23
  331.9 6.6 %collective-permute-start.27 = (f32[3,14,3,128]{3,2,1,0:T(4,128)S(1)}, f32[3,14,3,128]{3,2,1,0:T(4,128)S(1)}, u32[]{:S(2)}, u32[]{:S(2)}) collective-permute-start(f32[3,14,3,128]{3,2,1,0:T(4,128)S(1)} %get-tuple-element.1316), channel_id=1, source_target_pairs={{1,0},{2,1},{3,2},{4,3},{5,4},{6,5},{7,6},{9,8},{10,9},{11,10},{12... | collective-permute-start | bytes 193544 | tf_op jit(solution)/shard_map/ppermute | solution.py:25
  394.2 4.3 collective-permute-start.29
  399.5 6.6 %collective-permute-start.30 = (f32[3,14,3,128]{3,2,1,0:T(4,128)S(1)}, f32[3,14,3,128]{3,2,1,0:T(4,128)S(1)}, u32[]{:S(2)}, u32[]{:S(2)}) collective-permute-start(f32[3,14,3,128]{3,2,1,0:T(4,128)S(1)} %get-tuple-element.1311), channel_id=1, source_target_pairs={{0,1},{1,2},{2,3},{3,4},{4,5},{5,6},{6,7},{8,9},{9,10},{10,11},{11... | collective-permute-start | bytes 193544 | tf_op jit(solution)/shard_map/ppermute | solution.py:23
  403.7 6.6 %collective-permute-start.31 = (f32[3,14,3,128]{3,2,1,0:T(4,128)S(1)}, f32[3,14,3,128]{3,2,1,0:T(4,128)S(1)}, u32[]{:S(2)}, u32[]{:S(2)}) collective-permute-start(f32[3,14,3,128]{3,2,1,0:T(4,128)S(1)} %get-tuple-element.1312), channel_id=1, source_target_pairs={{1,0},{2,1},{3,2},{4,3},{5,4},{6,5},{7,6},{9,8},{10,9},{11,10},{12... | collective-permute-start | bytes 193544 | tf_op jit(solution)/shard_map/ppermute | solution.py:25
  465.2 4.3 collective-permute-start.33
  470.4 6.6 %collective-permute-start.34 = (f32[3,14,3,128]{3,2,1,0:T(4,128)S(1)}, f32[3,14,3,128]{3,2,1,0:T(4,128)S(1)}, u32[]{:S(2)}, u32[]{:S(2)}) collective-permute-start(f32[3,14,3,128]{3,2,1,0:T(4,128)S(1)} %get-tuple-element.1307), channel_id=1, source_target_pairs={{0,1},{1,2},{2,3},{3,4},{4,5},{5,6},{6,7},{8,9},{9,10},{10,11},{11... | collective-permute-start | bytes 193544 | tf_op jit(solution)/shard_map/ppermute | solution.py:23
  474.6 6.6 %collective-permute-start.35 = (f32[3,14,3,128]{3,2,1,0:T(4,128)S(1)}, f32[3,14,3,128]{3,2,1,0:T(4,128)S(1)}, u32[]{:S(2)}, u32[]{:S(2)}) collective-permute-start(f32[3,14,3,128]{3,2,1,0:T(4,128)S(1)} %get-tuple-element.1308), channel_id=1, source_target_pairs={{1,0},{2,1},{3,2},{4,3},{5,4},{6,5},{7,6},{9,8},{10,9},{11,10},{12... | collective-permute-start | bytes 193544 | tf_op jit(solution)/shard_map/ppermute | solution.py:25
  541.3 6.6 %collective-permute-start.38 = (f32[3,14,3,128]{3,2,1,0:T(4,128)S(1)}, f32[3,14,3,128]{3,2,1,0:T(4,128)S(1)}, u32[]{:S(2)}, u32[]{:S(2)}) collective-permute-start(f32[3,14,3,128]{3,2,1,0:T(4,128)S(1)} %get-tuple-element.1303), channel_id=1, source_target_pairs={{0,1},{1,2},{2,3},{3,4},{4,5},{5,6},{6,7},{8,9},{9,10},{10,11},{11... | collective-permute-start | bytes 193544 | tf_op jit(solution)/shard_map/ppermute | solution.py:23
  545.5 6.6 %collective-permute-start.39 = (f32[3,14,3,128]{3,2,1,0:T(4,128)S(1)}, f32[3,14,3,128]{3,2,1,0:T(4,128)S(1)}, u32[]{:S(2)}, u32[]{:S(2)}) collective-permute-start(f32[3,14,3,128]{3,2,1,0:T(4,128)S(1)} %get-tuple-element.1304), channel_id=1, source_target_pairs={{1,0},{2,1},{3,2},{4,3},{5,4},{6,5},{7,6},{9,8},{10,9},{11,10},{12... | collective-permute-start | bytes 193544 | tf_op jit(solution)/shard_map/ppermute | solution.py:25
  (27 other events, 312.4 us)
where the time goes:
time: 620 us; the launch traced here: 608 us
  blocking collectives  341 us (55%)
  other arithmetic  105 us (17%)
  starting transfers between devices  103 us (17%)
  waiting for transfers between devices  42.6 us (7%)
  between operations  14.4 us (2%)
    psum x8, blocking collectives, on_device(): lax.psum((jnp.sum(speed * speed), jnp.sum(speed * (previous - current))),...  341 us
    another operation x27, other arithmetic, bond_forces(): return jnp.stack(totals)  81.3 us
    ppermute x20, starting transfers between devices, extended(): lax.ppermute(tail, axis, [(i, (i + 1) % count) for i in range(ends)])  76.1 us
    ppermute x20, waiting for transfers between devices, extended(): lax.ppermute(head, axis, [((i + 1) % count, i) for i in range(ends)])  29.2 us
    ppermute x20, starting transfers between devices, extended(): lax.ppermute(head, axis, [((i + 1) % count, i) for i in range(ends)])  26.6 us
    ppermute x20, waiting for transfers between devices, extended(): lax.ppermute(tail, axis, [(i, (i + 1) % count) for i in range(ends)])  13.4 us
  transfers between devices with their start and end apart: 40, of which 22 were waited for; matrix products, arithmetic and copies ran while one was open for 1% of the time, Pallas kernels for 0%

commit v1 on v0

v1 whole, which is shorter than its diff:
```python
import math

import jax
import jax.numpy as jnp
from jax import lax
from jax.experimental import pallas as pl
from jax.experimental.pallas import tpu as pltpu
from jax.sharding import PartitionSpec as P

ITERS = 8
MASS = 64.0
EPS = 1e-06
LEAD = 8
VMEM = pltpu.CompilerParams(vmem_limit_bytes=48 * 1024 * 1024)


def neighbour_table():
    table = []
    for a in range(-3, 4):
        for b in range(-3, 4):
            for c in range(-3, 4):
                if 0 < a * a + b * b + c * c <= 9:
                    table.append((a, b, c))
    return table


TABLE = neighbour_table()
COLUMNS = [(a, b) for a in range(-3, 4) for b in range(-3, 4) if a * a + b * b <= 9]


def place(a, b, c):
    if abs(c) == 3:
        return 2 + (2 if c > 0 else -2), 29
    return 2 + c, COLUMNS.index((a, b))


def weight(a, b, c):
    length = float(a * a + b * b + c * c)
    return 1.0 / (length * math.sqrt(length) * MASS)


def shifted(x, axis, up):
    ends = lax.axis_size(axis) - 1
    if up:
        pairs = [(i, i + 1) for i in range(ends)]
    else:
        pairs = [(i + 1, i) for i in range(ends)]
    return lax.ppermute(x, axis, pairs)


def halos(q, outside=None):
    rows, cols = q.shape[1], q.shape[2]

    def edge(lo, hi, axis):
        if outside is None:
            return lo, hi
        at = lax.axis_index(axis)
        lo = jnp.where(at == 0, outside, lo)
        hi = jnp.where(at == lax.axis_size(axis) - 1, outside, hi)
        return lo, hi

    yl = shifted(q[:, :, cols - 3 :], "gy", True)
    yr = shifted(q[:, :, :3], "gy", False)
    yl, yr = edge(yl, yr, "gy")

    def strip(part):
        return jnp.concatenate([yl[:, part], q[:, part], yr[:, part]], axis=2)

    xl = shifted(strip(slice(rows - 3, rows)), "gx", True)
    xr = shifted(strip(slice(0, 3)), "gx", False)
    xl, xr = edge(xl, xr, "gx")
    return yl, yr, xl, xr


def fill(ext, q, yl, yr, xl, xr, shift):
    fields, rows, cols, depth = q.shape
    for f in range(fields):
        base = q[f, 0, 0:1, 0:1] if shift else None

        def moved(x):
            return x - base if shift else x

        ext[f, 3 : 3 + rows, LEAD : LEAD + cols, :] = moved(q[f])
        ext[f, 3 : 3 + rows, LEAD - 3 : LEAD, :] = moved(yl[f])
        ext[f, 3 : 3 + rows, LEAD + cols : LEAD + cols + 3, :] = moved(yr[f])
        ext[f, 0:3, LEAD - 3 : LEAD + cols + 3, :] = moved(xl[f])
        ext[f, 3 + rows :, LEAD - 3 : LEAD + cols + 3, :] = moved(xr[f])


def turn(x, by):
    depth = x.shape[-1]
    return pltpu.roll(x, by % depth, x.ndim - 1)


def prep_kernel(q, yl, yr, xl, xr, words_out, k_out, ext):
    _, rows, cols, depth = q.shape
    fill(ext, q, yl, yr, xl, xr, False)

    def row(r, carry):
        lane = lax.broadcasted_iota(jnp.int32, (8, depth), 1)
        for tile in range(cols // 8):
            at = pl.ds(tile * 8, 8)
            own = [q[w, r, at, :] for w in range(4)]
            bits = {c: jnp.zeros((8, depth), jnp.int32) for c in range(-3, 4)}
            ks = [jnp.zeros((8, depth), jnp.float32) for _ in range(6)]
            for number, (a, b, c) in enumerate(TABLE):
                word, bit = divmod(number, 31)
                mword, mbit = divmod(121 - number, 31)
                far = ext[mword, r + 3 + a, LEAD + tile * 8 + b : LEAD + tile * 8 + b + 8, :]
                if c:
                    far = turn(far, -c)
                broken = ((own[word] >> bit) | (far >> mbit)) & 1
                whole = broken == 0
                if c > 0:
                    whole = whole & (lane < depth - c)
                if c < 0:
                    whole = whole & (lane >= -c)
                slot = place(a, b, c)[1]
                bits[c] = bits[c] | jnp.where(whole, jnp.int32(1 << slot), 0)
                m = jnp.where(whole, jnp.float32(weight(a, b, c)), 0.0)
                for i, g in enumerate((a * a, b * b, c * c, a * b, a * c, b * c)):
                    if g:
                        ks[i] = ks[i] + (m if g == 1 else m * float(g))
            for c in range(-2, 3):
                value = turn(bits[c], c) if c else bits[c]
                if abs(c) == 2:
                    far = 3 if c > 0 else -3
                    value = value | turn(bits[far], far)
                words_out[2 + c, r, at, :] = value
            for i in range(6):
                k_out[i, r, at, :] = ks[i]
        return carry

    lax.fori_loop(0, rows, row, 0)


def plus(acc, x):
    return x if acc is None else acc + x


def forces(ext, words, k, r, tile, chains):
    at = pl.ds(tile * 8, 8)
    bits = [words[w, r, at, :] for w in range(5)]
    out = [[None, None, None] for _ in range(chains)]
    for group in ((0, 1, -1), (2, -2, 3, -3)):
        acc = {(ch, c): [None, None, None] for ch in range(chains) for c in group}
        for big in range(4):
            for wide in range(4):
                levels = [c for c in group if 0 < big * big + wide * wide + c * c <= 9]
                if not levels:
                    continue
                signs_a = (1, -1) if big else (1,)
                signs_b = (1, -1) if wide else (1,)
                t = {}
                for sa in signs_a:
                    for sb in signs_b:
                        a, b = sa * big, sb * wide
                        conds = {}
                        for c in levels:
                            w, bit = place(a, b, c)
                            conds[c] = (bits[w] & jnp.int32(1 << bit)) != 0
                        start = LEAD + tile * 8 + b
                        for ch in range(chains):
                            u = [
                                ext[3 * ch + i, r + 3 + a, start : start + 8, :]
                                for i in range(3)
                            ]
                            flat = None
                            if a:
                                flat = u[0] if a == 1 else u[0] * float(a)
                            if b:
                                side = u[1] if b == 1 else u[1] * float(b)
                                flat = side if flat is None else flat + side
                            for c in levels:
                                d = flat
                                if c:
                                    up = u[2] if abs(c) == 1 else u[2] * float(abs(c))
                                    if d is None:
                                        d = up if c > 0 else -up
                                    else:
                                        d = d + up if c > 0 else d - up
                                t[ch, c, sa, sb] = jnp.where(conds[c], d, 0.0)
                for ch in range(chains):
                    for c in levels:
                        w = weight(big, wide, c)
                        cell = acc[ch, c]
                        if big and wide:
                            p1 = t[ch, c, 1, 1] + t[ch, c, -1, 1]
                            q1 = t[ch, c, 1, 1] - t[ch, c, -1, 1]
                            p2 = t[ch, c, 1, -1] + t[ch, c, -1, -1]
                            q2 = t[ch, c, 1, -1] - t[ch, c, -1, -1]
                            total, dx, dy = p1 + p2, q1 + q2, p1 - p2
                        elif big:
                            total = t[ch, c, 1, 1] + t[ch, c, -1, 1]
                            dx, dy = t[ch, c, 1, 1] - t[ch, c, -1, 1], None
                        elif wide:
                            total = t[ch, c, 1, 1] + t[ch, c, 1, -1]
                            dx, dy = None, t[ch, c, 1, 1] - t[ch, c, 1, -1]
                        else:
                            total, dx, dy = t[ch, c, 1, 1], None, None
                        if dx is not None:
                            cell[0] = plus(cell[0], dx * (w * big))
                        if dy is not None:
                            cell[1] = plus(cell[1], dy * (w * wide))
                        if c:
                            cell[2] = plus(cell[2], total * (w * c))
        for ch in range(chains):
            for c in group:
                for i in range(3):
                    x = acc[ch, c][i]
                    if x is not None:
                        out[ch][i] = plus(out[ch][i], turn(x, -c) if c else x)
    for ch in range(chains):
        u = [ext[3 * ch + i, r + 3, LEAD + tile * 8 : LEAD + tile * 8 + 8, :] for i in range(3)]
        ks = [k[i, r, at, :] for i in range(6)]
        o = out[ch]
        o[0] = o[0] - (ks[0] * u[0] + ks[3] * u[1] + ks[4] * u[2])
        o[1] = o[1] - (ks[3] * u[0] + ks[1] * u[1] + ks[5] * u[2])
        o[2] = o[2] - (ks[4] * u[0] + ks[5] * u[1] + ks[2] * u[2])
    return out


def dot3(x, y):
    return x[0] * y[0] + x[1] * y[1] + x[2] * y[2]


def apply_kernel(kind, *refs):
    q, yl, yr, xl, xr, words, k = refs[:7]
    extra = refs[7:-3]
    q_out, sums, ext = refs[-3:]
    fields, rows, cols, depth = q.shape
    chains = fields // 3
    fill(ext, q, yl, yr, xl, xr, True)
    sums[...] = jnp.zeros_like(sums)

    def row(r, carry):
        for tile in range(cols // 8):
            at = pl.ds(tile * 8, 8)
            out = forces(ext, words, k, r, tile, chains)
            was = [[q[3 * ch + i, r, at, :] for i in range(3)] for ch in range(chains)]
            if kind == "first":
                load, flags = extra
                on = flags[r, at, :].astype(jnp.float32) * (1.0 / MASS)
                for i in range(3):
                    out[0][i] = out[0][i] + on * load[i, r, at, :]
            for ch in range(chains):
                for i in range(3):
                    q_out[3 * ch + i, r, at, :] = out[ch][i]
            y_old, y_new = was[0], out[0]
            if kind == "last":
                x_old = [extra[0][3 + i, r, at, :] for i in range(3)]
            else:
                x_old, x_new = was[1], out[1]
                sums[0] += dot3(x_old, x_old)
                sums[1] += dot3(x_old, x_new)
            if kind != "last":
                sums[3] += dot3(x_old, y_new)
            if kind != "first":
                sums[2] += dot3(x_old, y_old)
                sums[4] += dot3(y_old, y_old)
                sums[5] += dot3(y_old, y_new)
        return carry

    lax.fori_loop(0, rows, row, 0)


def hankel(p, q, moments, lift):
    a, b, c = moments
    total = None
    n = len(p)
    for order in range(2 * n - 1):
        pp = pq = qq = None
        for i in range(n):
            j = order - i
            if not 0 <= j < n:
                continue
            if p[i] is not None and p[j] is not None and i <= j:
                z = p[i] * p[j]
                pp = plus(pp, z + z if i < j else z)
            if q[i] is not None and q[j] is not None and i <= j:
                z = q[i] * q[j]
                qq = plus(qq, z + z if i < j else z)
            if p[i] is not None and q[j] is not None:
                z = p[i] * q[j]
                pq = plus(pq, z + z)
        for mine, table in ((pp, a), (pq, b), (qq, c)):
            if mine is not None:
                total = plus(total, mine * table[order + lift])
    return total


def added(x, y):
    if x is None:
        return y
    return x if y is None else x + y


def finish_kernel(count, rounds, *refs):
    m, disp, vel = refs[:3]
    qs = refs[3 : 3 + rounds]
    u_out, v_out = refs[-2:]
    rows, cols, depth = disp.shape[1:]

    def moment(step, which):
        at = 6 * step + which
        return m[at : at + 1, :]

    a, b, c = {}, {}, {}
    for s in range(rounds):
        a[2 * s], a[2 * s + 1] = moment(s, 0), moment(s, 1)
        b[2 * s] = moment(s, 3)
        if s:
            b[2 * s - 1] = moment(s, 2)
            c[2 * s - 2], c[2 * s - 1] = moment(s, 4), moment(s, 5)
    one = jnp.ones((1, depth), jnp.float32)
    p, q = [one], [None]
    r, t = [None], [one]
    up, uq = [None] * rounds, [None] * rounds
    for step in range(rounds):
        kinetic = hankel(p, q, (a, b, c), 0) * (1.0 / count)
        rayleigh = jnp.maximum(-hankel(p, q, (a, b, c), 1), 0.0) * (1.0 / count)
        damping = 2.0 * jnp.sqrt(rayleigh / (kinetic + EPS))
        beta = 2.0 / (2.0 + damping)
        alpha = (2.0 - damping) / (2.0 + damping)

        def mixed(own, other):
            own = own + [None] * (len(other) - len(own))
            return [
                added(
                    None if x is None else alpha * x, None if y is None else beta * y
                )
                for x, y in zip(own, other)
            ]

        p, q = mixed(p, r), mixed(q, t)
        for j in range(len(p)):
            up[j], uq[j] = added(up[j], p[j]), added(uq[j], q[j])
        r = [added(x, y) for x, y in zip(r + [None], [None] + p)]
        t = [added(x, y) for x, y in zip(t + [None], [None] + q)]
    p, q = p[:rounds], q[:rounds]

    def row(at_row, carry):
        for tile in range(cols // 8):
            at = pl.ds(tile * 8, 8)
            for i in range(3):
                u, v = disp[i, at_row, at, :], None
                for j in range(rounds):
                    x = vel[i, at_row, at, :] if j == 0 else qs[j - 1][3 + i, at_row, at, :]
                    y = qs[j][i, at_row, at, :]
                    u = u + up[j] * x + uq[j] * y
                    v = plus(v, p[j] * x + q[j] * y)
                u_out[i, at_row, at, :] = u
                v_out[i, at_row, at, :] = v
        return carry

    lax.fori_loop(0, rows, row, 0)


def summed(x):
    for axis in ("gx", "gy"):
        size = lax.axis_size(axis)
        if size & (size - 1):
            x = lax.psum(x, axis)
            continue
        step = 1
        while step < size:
            x = x + lax.ppermute(x, axis, [(i, i ^ step) for i in range(size)])
            step *= 2
    return x


def on_device(disp, vel, load, flags, mask_bits):
    _, rows, cols, depth = disp.shape
    count = 3.0 * rows * lax.axis_size("gx") * cols * lax.axis_size("gy") * depth
    f32, i32 = jnp.float32, jnp.int32

    def scratch(fields, kind):
        return [pltpu.VMEM((fields, rows + 6, cols + 2 * LEAD, depth), kind)]

    words, k = pl.pallas_call(
        prep_kernel,
        out_shape=(
            jax.ShapeDtypeStruct((5, rows, cols, depth), i32),
            jax.ShapeDtypeStruct((6, rows, cols, depth), f32),
        ),
        scratch_shapes=scratch(4, i32),
        compiler_params=VMEM,
        name="prep",
    )(mask_bits, *halos(mask_bits, -1))

    def applied_to(q, kind, *extra):
        fields = q.shape[0]

        def body(*refs):
            apply_kernel(kind, *refs)

        return pl.pallas_call(
            body,
            out_shape=(
                jax.ShapeDtypeStruct(q.shape, f32),
                jax.ShapeDtypeStruct((6, 8, depth), f32),
            ),
            scratch_shapes=scratch(fields, f32),
            compiler_params=VMEM,
            name="apply_" + kind,
        )(q, *halos(q), words, k, *extra)

    q, sums = applied_to(jnp.concatenate([disp, vel]), "first", load, flags)
    qs, parts = [q], [sums]
    for step in range(1, ITERS - 1):
        q, sums = applied_to(q, "mid")
        qs.append(q)
        parts.append(sums)
    last, sums = applied_to(q[:3], "last", q)
    qs.append(last)
    parts.append(sums)
    local = jnp.sum(jnp.stack(parts).reshape(6 * ITERS, 8 * depth), axis=1)
    moments = summed(jnp.pad(local, (0, 128 - 6 * ITERS)).reshape(1, 128))
    spread = jnp.broadcast_to(moments.reshape(128, 1)[: 6 * ITERS], (6 * ITERS, depth))

    def body(*refs):
        finish_kernel(count, ITERS, *refs)

    return pl.pallas_call(
        body,
        out_shape=(jax.ShapeDtypeStruct(disp.shape, f32), jax.ShapeDtypeStruct(vel.shape, f32)),
        compiler_params=VMEM,
        name="finish",
    )(spread, disp, vel, *qs)


def solution(mesh):
    placed = (
        P(None, "gx", "gy", None),
        P(None, "gx", "gy", None),
        P(None, "gx", "gy", None),
        P("gx", "gy", None),
        P(None, "gx", "gy", None),
    )
    return jax.shard_map(
        on_device,
        mesh=mesh,
        in_specs=placed,
        out_specs=(P(None, "gx", "gy", None), P(None, "gx", "gy", None)),
        check_vma=False,
    )
```

time: 620 us -> 218 us (0.35); the launches traced: 608 us -> 217 us
  blocking collectives: 341 us -> 0 us
  other arithmetic: 105 us -> 0.85 us
  Pallas kernels: 0 us -> 37.6 us
  starting transfers between devices: 103 us -> 118 us
  waiting for transfers between devices: 42.6 us -> 56.7 us
  between operations: 14.4 us -> 1.62 us
    psum x8 -> x0, blocking collectives: 341 us -> none  [on_device(): lax.psum((jnp.sum(speed * speed), jnp.sum(speed * (previous - current))),...]
    another operation x27 -> x0, other arithmetic: 81.3 us -> none  [bond_forces(): return jnp.stack(totals)]
    pallas_call x0 -> x10, Pallas kernels: none -> 37.6 us  [the longest x8 31.1 us: applied_to(): pl.pallas_call(body, out_shape=(jax.ShapeDtypeStruct(q.shape, f32), jax.S...]
    ppermute x40 -> x41, starting transfers between devices: 103 us -> 118 us  [the longest x36 110 us: shifted(): return lax.ppermute(x, axis, pairs)]
    ppermute x40 -> x41, waiting for transfers between devices: 42.6 us -> 56.7 us  [the longest x36 43.6 us: shifted(): return lax.ppermute(x, axis, pairs)]
  transfers between devices with their start and end apart: 40 -> 41, of which waited for: 22 -> 26; matrix products, arithmetic and copies ran while one was open for 1% -> 0% of each run, Pallas kernels for 0% -> 2%
where the time goes in v1:
time: 218 us; the launch traced here: 217 us
  starting transfers between devices  118 us (54%)
  waiting for transfers between devices  56.7 us (26%)
  Pallas kernels  37.6 us (17%)
    ppermute x36, starting transfers between devices, shifted(): return lax.ppermute(x, axis, pairs)  110 us
    ppermute x36, waiting for transfers between devices, shifted(): return lax.ppermute(x, axis, pairs)  43.6 us
    pallas_call x8, Pallas kernels, applied_to(): pl.pallas_call(body, out_shape=(jax.ShapeDtypeStruct(q.shape, f32), jax.S...  31.1 us
    ppermute x5, waiting for transfers between devices, summed(): x = x + lax.ppermute(x, axis, [(i, i ^ step) for i in range(size)])  13.1 us
    ppermute x5, starting transfers between devices, summed(): x = x + lax.ppermute(x, axis, [(i, i ^ step) for i in range(size)])  8.33 us
    pallas_call x1, Pallas kernels, on_device(): pl.pallas_call(prep_kernel, out_shape=(jax.ShapeDtypeStruct((5, rows, col...  4.68 us
  transfers between devices with their start and end apart: 41, of which 26 were waited for; matrix products, arithmetic and copies ran while one was open for 0% of the time, Pallas kernels for 2%

profile of v1, /device:TPU:0, one launch (start us, length us, event | category | flops | bytes accessed | tf_op | source)
XLA Modules:
  0.0 216.7 jit_solution(17485081918346544969)
XLA Ops:
  1.7 4.9 %collective-permute-start.4 = (s32[4,8,3,128]{3,2,1,0:T(4,128)S(1)}, s32[4,8,3,128]{3,2,1,0:T(4,128)S(1)}, u32[]{:S(2)}, u32[]{:S(2)}) collective-permute-start(s32[4,8,3,128]{3,2,1,0:T(4,128)S(1)} %get-tuple-element.73), channel_id=1, source_target_pairs={{0,1},{1,2},{2,3},{3,4},{4,5},{5,6},{6,7},{8,9},{9,10},{10,11},{11... | collective-permute-start | bytes 147464 | tf_op jit(solution)/shard_map/ppermute | solution.py:48
  9.4 5.3 %collective-permute-start = (f32[6,8,3,128]{3,2,1,0:T(4,128)S(1)}, f32[6,8,3,128]{3,2,1,0:T(4,128)S(1)}, u32[]{:S(2)}, u32[]{:S(2)}) collective-permute-start(f32[6,8,3,128]{3,2,1,0:T(4,128)S(1)} %get-tuple-element.69), channel_id=1, source_target_pairs={{0,1},{1,2},{2,3},{3,4},{4,5},{5,6},{6,7},{8,9},{9,10},{10,11},{11... | collective-permute-start | bytes 221192 | tf_op jit(solution)/shard_map/ppermute | solution.py:48
  20.8 3.7 %collective-permute-start.2 = (f32[6,3,22,128]{3,2,1,0:T(8,128)S(1)}, f32[6,3,22,128]{3,2,1,0:T(8,128)S(1)}, u32[]{:S(2)}, u32[]{:S(2)}) collective-permute-start(f32[6,3,22,128]{3,2,1,0:T(8,128)S(1)} %pad_maximum_fusion), channel_id=1, source_target_pairs={{0,8},{8,16},{16,24},{1,9},{9,17},{17,25},{2,10},{10,18},{18,26},{... | collective-permute-start | bytes 608264 | tf_op jit(solution)/shard_map/ppermute | solution.py:48
  24.6 4.7 %prep.1 = (s32[5,8,16,128]{3,2,1,0:T(8,128)S(1)}, f32[6,8,16,128]{3,2,1,0:T(8,128)S(1)}) custom-call(s32[4,8,16,128]{3,2,1,0:T(8,128)S(1)} %copy-done, s32[4,8,3,128]{3,2,1,0:T(4,128)S(1)} %broadcast_select_fusion.3.yl, s32[4,8,3,128]{3,2,1,0:T(4,128)S(1)} %broadcast_select_fusion.2.yr, s32[4,3,22,128]{3,2,1,0:T(8,128)S(1)} %broadcast_select_fusion.1.xl, ...), custom_call_target="tpu_custom_call" | custom-call | tf_op jit(solution)/shard_map/prep/pallas_call | solution.py:380
  29.3 4.1 %apply_first.1 = (f32[6,8,16,128]{3,2,1,0:T(8,128)S(1)}, f32[6,8,128]{2,1,0:T(8,128)S(1)}) custom-call(f32[6,8,16,128]{3,2,1,0:T(8,128)S(1)} %constant_dynamic-update-slice_fusion.refs_0_, f32[6,8,3,128]{3,2,1,0:T(4,128)S(1)} %collective-permute-done.refs_1_, f32[6,8,3,128]{3,2,1,0:T(4,128)S(1)} %collective-permute-done.1.refs_2_, ...), custom_call_target="tpu_custom_call" | custom-call | tf_op jit(solution)/shard_map/apply_first/pallas_call | solution.py:397
  33.5 4.8 %collective-permute-start.8 = (f32[6,8,3,128]{3,2,1,0:T(4,128)S(1)}, f32[6,8,3,128]{3,2,1,0:T(4,128)S(1)}, u32[]{:S(2)}, u32[]{:S(2)}) collective-permute-start(f32[6,8,3,128]{3,2,1,0:T(4,128)S(1)} %get-tuple-element.65), channel_id=1, source_target_pairs={{0,1},{1,2},{2,3},{3,4},{4,5},{5,6},{6,7},{8,9},{9,10},{10,11},{11... | collective-permute-start | bytes 221192 | tf_op jit(solution)/shard_map/ppermute | solution.py:48
  40.7 4.7 %collective-permute-done.9.refs_2_ = f32[6,8,3,128]{3,2,1,0:T(4,128)S(1)} collective-permute-done((f32[6,8,3,128]{3,2,1,0:T(4,128)S(1)}, f32[6,8,3,128]{3,2,1,0:T(4,128)S(1)}, u32[]{:S(2)}, u32[]{:S(2)}) %collective-permute-start.9) | collective-permute-done | bytes 73760 | tf_op jit(solution)/shard_map/ppermute | solution.py:48
  50.9 4.1 %apply_mid.6 = (f32[6,8,16,128]{3,2,1,0:T(8,128)S(1)}, f32[6,8,128]{2,1,0:T(8,128)S(1)}) custom-call(f32[6,8,16,128]{3,2,1,0:T(8,128)S(1)} %get-tuple-element.23.refs_0_.refs_3_, f32[6,8,3,128]{3,2,1,0:T(4,128)S(1)} %collective-permute-done.8.refs_1_, f32[6,8,3,128]{3,2,1,0:T(4,128)S(1)} %collective-permute-done.9.refs_2_, ...), custom_call_target="tpu_custom_call" | custom-call | tf_op jit(solution)/shard_map/apply_mid/pallas_call | solution.py:397
  55.1 4.4 %collective-permute-start.12 = (f32[6,8,3,128]{3,2,1,0:T(4,128)S(1)}, f32[6,8,3,128]{3,2,1,0:T(4,128)S(1)}, u32[]{:S(2)}, u32[]{:S(2)}) collective-permute-start(f32[6,8,3,128]{3,2,1,0:T(4,128)S(1)} %get-tuple-element.61), channel_id=1, source_target_pairs={{0,1},{1,2},{2,3},{3,4},{4,5},{5,6},{6,7},{8,9},{9,10},{10,11},{11... | collective-permute-start | bytes 221192 | tf_op jit(solution)/shard_map/ppermute | solution.py:48
  61.7 4.3 %collective-permute-done.13.refs_2_ = f32[6,8,3,128]{3,2,1,0:T(4,128)S(1)} collective-permute-done((f32[6,8,3,128]{3,2,1,0:T(4,128)S(1)}, f32[6,8,3,128]{3,2,1,0:T(4,128)S(1)}, u32[]{:S(2)}, u32[]{:S(2)}) %collective-permute-start.13) | collective-permute-done | bytes 73760 | tf_op jit(solution)/shard_map/ppermute | solution.py:48
  67.4 4.4 %collective-permute-start.14 = (f32[6,3,22,128]{3,2,1,0:T(8,128)S(1)}, f32[6,3,22,128]{3,2,1,0:T(8,128)S(1)}, u32[]{:S(2)}, u32[]{:S(2)}) collective-permute-start(f32[6,3,22,128]{3,2,1,0:T(8,128)S(1)} %pad_maximum_fusion.4), channel_id=1, source_target_pairs={{0,8},{8,16},{16,24},{1,9},{9,17},{17,25},{2,10},{10,18},{18,26},{... | collective-permute-start | bytes 608264 | tf_op jit(solution)/shard_map/ppermute | solution.py:48
  72.9 4.1 %apply_mid.7 = (f32[6,8,16,128]{3,2,1,0:T(8,128)S(1)}, f32[6,8,128]{2,1,0:T(8,128)S(1)}) custom-call(f32[6,8,16,128]{3,2,1,0:T(8,128)S(1)} %get-tuple-element.25.refs_0_.refs_4_, f32[6,8,3,128]{3,2,1,0:T(4,128)S(1)} %collective-permute-done.12.refs_1_, f32[6,8,3,128]{3,2,1,0:T(4,128)S(1)} %collective-permute-done.13.refs_2_, ...), custom_call_target="tpu_custom_call" | custom-call | tf_op jit(solution)/shard_map/apply_mid/pallas_call | solution.py:397
  82.7 4.3 %collective-permute-done.17.refs_2_ = f32[6,8,3,128]{3,2,1,0:T(4,128)S(1)} collective-permute-done((f32[6,8,3,128]{3,2,1,0:T(4,128)S(1)}, f32[6,8,3,128]{3,2,1,0:T(4,128)S(1)}, u32[]{:S(2)}, u32[]{:S(2)}) %collective-permute-start.17) | collective-permute-done | bytes 73760 | tf_op jit(solution)/shard_map/ppermute | solution.py:48
  88.4 6.8 %collective-permute-start.18 = (f32[6,3,22,128]{3,2,1,0:T(8,128)S(1)}, f32[6,3,22,128]{3,2,1,0:T(8,128)S(1)}, u32[]{:S(2)}, u32[]{:S(2)}) collective-permute-start(f32[6,3,22,128]{3,2,1,0:T(8,128)S(1)} %pad_maximum_fusion.6), channel_id=1, source_target_pairs={{0,8},{8,16},{16,24},{1,9},{9,17},{17,25},{2,10},{10,18},{18,26},{... | collective-permute-start | bytes 608264 | tf_op jit(solution)/shard_map/ppermute | solution.py:48
  96.3 4.1 %apply_mid.8 = (f32[6,8,16,128]{3,2,1,0:T(8,128)S(1)}, f32[6,8,128]{2,1,0:T(8,128)S(1)}) custom-call(f32[6,8,16,128]{3,2,1,0:T(8,128)S(1)} %get-tuple-element.27.refs_0_.refs_5_, f32[6,8,3,128]{3,2,1,0:T(4,128)S(1)} %collective-permute-done.16.refs_1_, f32[6,8,3,128]{3,2,1,0:T(4,128)S(1)} %collective-permute-done.17.refs_2_, ...), custom_call_target="tpu_custom_call" | custom-call | tf_op jit(solution)/shard_map/apply_mid/pallas_call | solution.py:397
  100.4 4.4 %collective-permute-start.20 = (f32[6,8,3,128]{3,2,1,0:T(4,128)S(1)}, f32[6,8,3,128]{3,2,1,0:T(4,128)S(1)}, u32[]{:S(2)}, u32[]{:S(2)}) collective-permute-start(f32[6,8,3,128]{3,2,1,0:T(4,128)S(1)} %get-tuple-element.53), channel_id=1, source_target_pairs={{0,1},{1,2},{2,3},{3,4},{4,5},{5,6},{6,7},{8,9},{9,10},{10,11},{11... | collective-permute-start | bytes 221192 | tf_op jit(solution)/shard_map/ppermute | solution.py:48
  107.0 4.3 %collective-permute-done.21.refs_2_ = f32[6,8,3,128]{3,2,1,0:T(4,128)S(1)} collective-permute-done((f32[6,8,3,128]{3,2,1,0:T(4,128)S(1)}, f32[6,8,3,128]{3,2,1,0:T(4,128)S(1)}, u32[]{:S(2)}, u32[]{:S(2)}) %collective-permute-start.21) | collective-permute-done | bytes 73760 | tf_op jit(solution)/shard_map/ppermute | solution.py:48
  112.8 6.8 %collective-permute-start.22 = (f32[6,3,22,128]{3,2,1,0:T(8,128)S(1)}, f32[6,3,22,128]{3,2,1,0:T(8,128)S(1)}, u32[]{:S(2)}, u32[]{:S(2)}) collective-permute-start(f32[6,3,22,128]{3,2,1,0:T(8,128)S(1)} %pad_maximum_fusion.8), channel_id=1, source_target_pairs={{0,8},{8,16},{16,24},{1,9},{9,17},{17,25},{2,10},{10,18},{18,26},{... | collective-permute-start | bytes 608264 | tf_op jit(solution)/shard_map/ppermute | solution.py:48
  120.6 4.1 %apply_mid.9 = (f32[6,8,16,128]{3,2,1,0:T(8,128)S(1)}, f32[6,8,128]{2,1,0:T(8,128)S(1)}) custom-call(f32[6,8,16,128]{3,2,1,0:T(8,128)S(1)} %get-tuple-element.29.refs_0_.refs_6_, f32[6,8,3,128]{3,2,1,0:T(4,128)S(1)} %collective-permute-done.20.refs_1_, f32[6,8,3,128]{3,2,1,0:T(4,128)S(1)} %collective-permute-done.21.refs_2_, ...), custom_call_target="tpu_custom_call" | custom-call | tf_op jit(solution)/shard_map/apply_mid/pallas_call | solution.py:397
  124.8 3.4 %collective-permute-start.24 = (f32[6,8,3,128]{3,2,1,0:T(4,128)S(1)}, f32[6,8,3,128]{3,2,1,0:T(4,128)S(1)}, u32[]{:S(2)}, u32[]{:S(2)}) collective-permute-start(f32[6,8,3,128]{3,2,1,0:T(4,128)S(1)} %get-tuple-element.49), channel_id=1, source_target_pairs={{0,1},{1,2},{2,3},{3,4},{4,5},{5,6},{6,7},{8,9},{9,10},{10,11},{11... | collective-permute-start | bytes 221192 | tf_op jit(solution)/shard_map/ppermute | solution.py:48
  130.4 4.3 %collective-permute-done.25.refs_2_ = f32[6,8,3,128]{3,2,1,0:T(4,128)S(1)} collective-permute-done((f32[6,8,3,128]{3,2,1,0:T(4,128)S(1)}, f32[6,8,3,128]{3,2,1,0:T(4,128)S(1)}, u32[]{:S(2)}, u32[]{:S(2)}) %collective-permute-start.25) | collective-permute-done | bytes 73760 | tf_op jit(solution)/shard_map/ppermute | solution.py:48
  136.1 6.8 %collective-permute-start.26 = (f32[6,3,22,128]{3,2,1,0:T(8,128)S(1)}, f32[6,3,22,128]{3,2,1,0:T(8,128)S(1)}, u32[]{:S(2)}, u32[]{:S(2)}) collective-permute-start(f32[6,3,22,128]{3,2,1,0:T(8,128)S(1)} %pad_maximum_fusion.10), channel_id=1, source_target_pairs={{0,8},{8,16},{16,24},{1,9},{9,17},{17,25},{2,10},{10,18},{18,26},{... | collective-permute-start | bytes 608264 | tf_op jit(solution)/shard_map/ppermute | solution.py:48
  144.0 4.1 %apply_mid.10 = (f32[6,8,16,128]{3,2,1,0:T(8,128)S(1)}, f32[6,8,128]{2,1,0:T(8,128)S(1)}) custom-call(f32[6,8,16,128]{3,2,1,0:T(8,128)S(1)} %get-tuple-element.31.refs_0_.refs_7_, f32[6,8,3,128]{3,2,1,0:T(4,128)S(1)} %collective-permute-done.24.refs_1_, f32[6,8,3,128]{3,2,1,0:T(4,128)S(1)} %collective-permute-done.25.refs_2_, ...), custom_call_target="tpu_custom_call" | custom-call | tf_op jit(solution)/shard_map/apply_mid/pallas_call | solution.py:397
  148.2 4.4 %collective-permute-start.28 = (f32[6,8,3,128]{3,2,1,0:T(4,128)S(1)}, f32[6,8,3,128]{3,2,1,0:T(4,128)S(1)}, u32[]{:S(2)}, u32[]{:S(2)}) collective-permute-start(f32[6,8,3,128]{3,2,1,0:T(4,128)S(1)} %get-tuple-element.45), channel_id=1, source_target_pairs={{0,1},{1,2},{2,3},{3,4},{4,5},{5,6},{6,7},{8,9},{9,10},{10,11},{11... | collective-permute-start | bytes 221192 | tf_op jit(solution)/shard_map/ppermute | solution.py:48
  154.7 4.3 %collective-permute-done.29.refs_2_ = f32[6,8,3,128]{3,2,1,0:T(4,128)S(1)} collective-permute-done((f32[6,8,3,128]{3,2,1,0:T(4,128)S(1)}, f32[6,8,3,128]{3,2,1,0:T(4,128)S(1)}, u32[]{:S(2)}, u32[]{:S(2)}) %collective-permute-start.29) | collective-permute-done | bytes 73760 | tf_op jit(solution)/shard_map/ppermute | solution.py:48
  160.5 6.8 %collective-permute-start.30 = (f32[6,3,22,128]{3,2,1,0:T(8,128)S(1)}, f32[6,3,22,128]{3,2,1,0:T(8,128)S(1)}, u32[]{:S(2)}, u32[]{:S(2)}) collective-permute-start(f32[6,3,22,128]{3,2,1,0:T(8,128)S(1)} %pad_maximum_fusion.12), channel_id=1, source_target_pairs={{0,8},{8,16},{16,24},{1,9},{9,17},{17,25},{2,10},{10,18},{18,26},{... | collective-permute-start | bytes 608264 | tf_op jit(solution)/shard_map/ppermute | solution.py:48
  168.4 4.1 %apply_mid.11 = (f32[6,8,16,128]{3,2,1,0:T(8,128)S(1)}, f32[6,8,128]{2,1,0:T(8,128)S(1)}) custom-call(f32[6,8,16,128]{3,2,1,0:T(8,128)S(1)} %get-tuple-element.33.refs_0_.refs_8_, f32[6,8,3,128]{3,2,1,0:T(4,128)S(1)} %collective-permute-done.28.refs_1_, f32[6,8,3,128]{3,2,1,0:T(4,128)S(1)} %collective-permute-done.29.refs_2_, ...), custom_call_target="tpu_custom_call" | custom-call | tf_op jit(solution)/shard_map/apply_mid/pallas_call | solution.py:397
  177.4 4.3 %collective-permute-done.33.refs_2_ = f32[3,8,3,128]{3,2,1,0:T(4,128)S(1)} collective-permute-done((f32[3,8,3,128]{3,2,1,0:T(4,128)S(1)}, f32[3,8,3,128]{3,2,1,0:T(4,128)S(1)}, u32[]{:S(2)}, u32[]{:S(2)}) %collective-permute-start.33) | collective-permute-done | bytes 36896 | tf_op jit(solution)/shard_map/ppermute | solution.py:48
  183.1 6.8 %collective-permute-start.34 = (f32[3,3,22,128]{3,2,1,0:T(8,128)S(1)}, f32[3,3,22,128]{3,2,1,0:T(8,128)S(1)}, u32[]{:S(2)}, u32[]{:S(2)}) collective-permute-start(f32[3,3,22,128]{3,2,1,0:T(8,128)S(1)} %pad_maximum_fusion.14), channel_id=1, source_target_pairs={{0,8},{8,16},{16,24},{1,9},{9,17},{17,25},{2,10},{10,18},{18,26},{... | collective-permute-start | bytes 304136 | tf_op jit(solution)/shard_map/ppermute | solution.py:48
  193.4 4.8 %collective-permute-start.36 = (f32[1,128]{1,0:T(1,128)S(1)}, f32[1,128]{1,0:T(1,128)S(1)}, u32[]{:S(2)}, u32[]{:S(2)}) collective-permute-start(f32[1,128]{1,0:T(1,128)S(1)} %pad_bitcast_fusion), channel_id=1, source_target_pairs={{0,8},{8,0},{16,24},{24,16},{1,9},{9,1},{17,25},{25,17},{2,10},{10... | collective-permute-start | bytes 1544 | tf_op jit(solution)/shard_map/ppermute | solution.py:367
  206.8 3.6 %collective-permute-done.39 = f32[1,128]{1,0:T(1,128)S(1)} collective-permute-done((f32[1,128]{1,0:T(1,128)S(1)}, f32[1,128]{1,0:T(1,128)S(1)}, u32[]{:S(2)}, u32[]{:S(2)}) %collective-permute-start.39) | collective-permute-done | bytes 544 | tf_op jit(solution)/shard_map/ppermute | solution.py:367
  210.4 4.5 %collective-permute-done.40 = f32[1,128]{1,0:T(1,128)S(1)} collective-permute-done((f32[1,128]{1,0:T(1,128)S(1)}, f32[1,128]{1,0:T(1,128)S(1)}, u32[]{:S(2)}, u32[]{:S(2)}) %collective-permute-start.40) | collective-permute-done | bytes 544 | tf_op jit(solution)/shard_map/ppermute | solution.py:367
  (149 shorter events, 64.7 us)
Async XLA Ops:
  1.7 13.1 %collective-permute-start.4 = (s32[4,8,3,128]{3,2,1,0:T(4,128)S(1)}, s32[4,8,3,128]{3,2,1,0:T(4,128)S(1)}, u32[]{:S(2)}, u32[]{:S(2)}) collective-permute-start(s32[4,8,3,128]{3,2,1,0:T(4,128)S(1)} %get-tuple-element.73), channel_id=1, source_target_pairs={{0,1},{1,2},{2,3},{3,4},{4,5},{5,6},{6,7},{8,9},{9,10},{10,11},{11... | collective-permute-start | bytes 147464 | tf_op jit(solution)/shard_map/ppermute | solution.py:48
  6.6 8.3 %collective-permute-start.5 = (s32[4,8,3,128]{3,2,1,0:T(4,128)S(1)}, s32[4,8,3,128]{3,2,1,0:T(4,128)S(1)}, u32[]{:S(2)}, u32[]{:S(2)}) collective-permute-start(s32[4,8,3,128]{3,2,1,0:T(4,128)S(1)} %get-tuple-element.72), channel_id=1, source_target_pairs={{1,0},{2,1},{3,2},{4,3},{5,4},{6,5},{7,6},{9,8},{10,9},{11,10},{12... | collective-permute-start | bytes 147464 | tf_op jit(solution)/shard_map/ppermute | solution.py:48
  8.1 11.2 %collective-permute-start.1 = (f32[6,8,3,128]{3,2,1,0:T(4,128)S(1)}, f32[6,8,3,128]{3,2,1,0:T(4,128)S(1)}, u32[]{:S(2)}, u32[]{:S(2)}) collective-permute-start(f32[6,8,3,128]{3,2,1,0:T(4,128)S(1)} %get-tuple-element.68), channel_id=1, source_target_pairs={{1,0},{2,1},{3,2},{4,3},{5,4},{6,5},{7,6},{9,8},{10,9},{11,10},{12... | collective-permute-start | bytes 221192 | tf_op jit(solution)/shard_map/ppermute | solution.py:48
  9.4 9.9 %collective-permute-start = (f32[6,8,3,128]{3,2,1,0:T(4,128)S(1)}, f32[6,8,3,128]{3,2,1,0:T(4,128)S(1)}, u32[]{:S(2)}, u32[]{:S(2)}) collective-permute-start(f32[6,8,3,128]{3,2,1,0:T(4,128)S(1)} %get-tuple-element.69), channel_id=1, source_target_pairs={{0,1},{1,2},{2,3},{3,4},{4,5},{5,6},{6,7},{8,9},{9,10},{10,11},{11... | collective-permute-start | bytes 221192 | tf_op jit(solution)/shard_map/ppermute | solution.py:48
  15.0 9.5 %collective-permute-start.7 = (s32[4,3,22,128]{3,2,1,0:T(8,128)S(1)}, s32[4,3,22,128]{3,2,1,0:T(8,128)S(1)}, u32[]{:S(2)}, u32[]{:S(2)}) collective-permute-start(s32[4,3,22,128]{3,2,1,0:T(8,128)S(1)} %pad_add_fusion.1), channel_id=1, source_target_pairs={{8,0},{16,8},{24,16},{9,1},{17,9},{25,17},{10,2},{18,10},{26,18},{... | collective-permute-start | bytes 405512 | tf_op jit(solution)/shard_map/ppermute | solution.py:48
  16.3 8.2 %collective-permute-start.6 = (s32[4,3,22,128]{3,2,1,0:T(8,128)S(1)}, s32[4,3,22,128]{3,2,1,0:T(8,128)S(1)}, u32[]{:S(2)}, u32[]{:S(2)}) collective-permute-start(s32[4,3,22,128]{3,2,1,0:T(8,128)S(1)} %pad_add_fusion), channel_id=1, source_target_pairs={{0,8},{8,16},{16,24},{1,9},{9,17},{17,25},{2,10},{10,18},{18,26},{... | collective-permute-start | bytes 405512 | tf_op jit(solution)/shard_map/ppermute | solution.py:48
  19.4 9.8 %collective-permute-start.3 = (f32[6,3,22,128]{3,2,1,0:T(8,128)S(1)}, f32[6,3,22,128]{3,2,1,0:T(8,128)S(1)}, u32[]{:S(2)}, u32[]{:S(2)}) collective-permute-start(f32[6,3,22,128]{3,2,1,0:T(8,128)S(1)} %pad_maximum_fusion.1), channel_id=1, source_target_pairs={{8,0},{16,8},{24,16},{9,1},{17,9},{25,17},{10,2},{18,10},{26,18},{... | collective-permute-start | bytes 608264 | tf_op jit(solution)/shard_map/ppermute | solution.py:48
  20.8 8.5 %collective-permute-start.2 = (f32[6,3,22,128]{3,2,1,0:T(8,128)S(1)}, f32[6,3,22,128]{3,2,1,0:T(8,128)S(1)}, u32[]{:S(2)}, u32[]{:S(2)}) collective-permute-start(f32[6,3,22,128]{3,2,1,0:T(8,128)S(1)} %pad_maximum_fusion), channel_id=1, source_target_pairs={{0,8},{8,16},{16,24},{1,9},{9,17},{17,25},{2,10},{10,18},{18,26},{... | collective-permute-start | bytes 608264 | tf_op jit(solution)/shard_map/ppermute | solution.py:48
  33.5 7.2 %collective-permute-start.8 = (f32[6,8,3,128]{3,2,1,0:T(4,128)S(1)}, f32[6,8,3,128]{3,2,1,0:T(4,128)S(1)}, u32[]{:S(2)}, u32[]{:S(2)}) collective-permute-start(f32[6,8,3,128]{3,2,1,0:T(4,128)S(1)} %get-tuple-element.65), channel_id=1, source_target_pairs={{0,1},{1,2},{2,3},{3,4},{4,5},{5,6},{6,7},{8,9},{9,10},{10,11},{11... | collective-permute-start | bytes 221192 | tf_op jit(solution)/shard_map/ppermute | solution.py:48
  38.3 7.1 %collective-permute-start.9 = (f32[6,8,3,128]{3,2,1,0:T(4,128)S(1)}, f32[6,8,3,128]{3,2,1,0:T(4,128)S(1)}, u32[]{:S(2)}, u32[]{:S(2)}) collective-permute-start(f32[6,8,3,128]{3,2,1,0:T(4,128)S(1)} %get-tuple-element.64), channel_id=1, source_target_pairs={{1,0},{2,1},{3,2},{4,3},{5,4},{6,5},{7,6},{9,8},{10,9},{11,10},{12... | collective-permute-start | bytes 221192 | tf_op jit(solution)/shard_map/ppermute | solution.py:48
  55.1 6.6 %collective-permute-start.12 = (f32[6,8,3,128]{3,2,1,0:T(4,128)S(1)}, f32[6,8,3,128]{3,2,1,0:T(4,128)S(1)}, u32[]{:S(2)}, u32[]{:S(2)}) collective-permute-start(f32[6,8,3,128]{3,2,1,0:T(4,128)S(1)} %get-tuple-element.61), channel_id=1, source_target_pairs={{0,1},{1,2},{2,3},{3,4},{4,5},{5,6},{6,7},{8,9},{9,10},{10,11},{11... | collective-permute-start | bytes 221192 | tf_op jit(solution)/shard_map/ppermute | solution.py:48
  59.5 6.5 %collective-permute-start.13 = (f32[6,8,3,128]{3,2,1,0:T(4,128)S(1)}, f32[6,8,3,128]{3,2,1,0:T(4,128)S(1)}, u32[]{:S(2)}, u32[]{:S(2)}) collective-permute-start(f32[6,8,3,128]{3,2,1,0:T(4,128)S(1)} %get-tuple-element.60), channel_id=1, source_target_pairs={{1,0},{2,1},{3,2},{4,3},{5,4},{6,5},{7,6},{9,8},{10,9},{11,10},{12... | collective-permute-start | bytes 221192 | tf_op jit(solution)/shard_map/ppermute | solution.py:48
  66.1 5.8 %collective-permute-start.15 = (f32[6,3,22,128]{3,2,1,0:T(8,128)S(1)}, f32[6,3,22,128]{3,2,1,0:T(8,128)S(1)}, u32[]{:S(2)}, u32[]{:S(2)}) collective-permute-start(f32[6,3,22,128]{3,2,1,0:T(8,128)S(1)} %pad_maximum_fusion.5), channel_id=1, source_target_pairs={{8,0},{16,8},{24,16},{9,1},{17,9},{25,17},{10,2},{18,10},{26,18},{... | collective-permute-start | bytes 608264 | tf_op jit(solution)/shard_map/ppermute | solution.py:48
  77.1 5.6 %collective-permute-start.16 = (f32[6,8,3,128]{3,2,1,0:T(4,128)S(1)}, f32[6,8,3,128]{3,2,1,0:T(4,128)S(1)}, u32[]{:S(2)}, u32[]{:S(2)}) collective-permute-start(f32[6,8,3,128]{3,2,1,0:T(4,128)S(1)} %get-tuple-element.57), channel_id=1, source_target_pairs={{0,1},{1,2},{2,3},{3,4},{4,5},{5,6},{6,7},{8,9},{9,10},{10,11},{11... | collective-permute-start | bytes 221192 | tf_op jit(solution)/shard_map/ppermute | solution.py:48
  80.5 6.5 %collective-permute-start.17 = (f32[6,8,3,128]{3,2,1,0:T(4,128)S(1)}, f32[6,8,3,128]{3,2,1,0:T(4,128)S(1)}, u32[]{:S(2)}, u32[]{:S(2)}) collective-permute-start(f32[6,8,3,128]{3,2,1,0:T(4,128)S(1)} %get-tuple-element.56), channel_id=1, source_target_pairs={{1,0},{2,1},{3,2},{4,3},{5,4},{6,5},{7,6},{9,8},{10,9},{11,10},{12... | collective-permute-start | bytes 221192 | tf_op jit(solution)/shard_map/ppermute | solution.py:48
  87.1 8.2 %collective-permute-start.19 = (f32[6,3,22,128]{3,2,1,0:T(8,128)S(1)}, f32[6,3,22,128]{3,2,1,0:T(8,128)S(1)}, u32[]{:S(2)}, u32[]{:S(2)}) collective-permute-start(f32[6,3,22,128]{3,2,1,0:T(8,128)S(1)} %pad_maximum_fusion.7), channel_id=1, source_target_pairs={{8,0},{16,8},{24,16},{9,1},{17,9},{25,17},{10,2},{18,10},{26,18},{... | collective-permute-start | bytes 608264 | tf_op jit(solution)/shard_map/ppermute | solution.py:48
  88.4 7.9 %collective-permute-start.18 = (f32[6,3,22,128]{3,2,1,0:T(8,128)S(1)}, f32[6,3,22,128]{3,2,1,0:T(8,128)S(1)}, u32[]{:S(2)}, u32[]{:S(2)}) collective-permute-start(f32[6,3,22,128]{3,2,1,0:T(8,128)S(1)} %pad_maximum_fusion.6), channel_id=1, source_target_pairs={{0,8},{8,16},{16,24},{1,9},{9,17},{17,25},{2,10},{10,18},{18,26},{... | collective-permute-start | bytes 608264 | tf_op jit(solution)/shard_map/ppermute | solution.py:48
  100.4 6.6 %collective-permute-start.20 = (f32[6,8,3,128]{3,2,1,0:T(4,128)S(1)}, f32[6,8,3,128]{3,2,1,0:T(4,128)S(1)}, u32[]{:S(2)}, u32[]{:S(2)}) collective-permute-start(f32[6,8,3,128]{3,2,1,0:T(4,128)S(1)} %get-tuple-element.53), channel_id=1, source_target_pairs={{0,1},{1,2},{2,3},{3,4},{4,5},{5,6},{6,7},{8,9},{9,10},{10,11},{11... | collective-permute-start | bytes 221192 | tf_op jit(solution)/shard_map/ppermute | solution.py:48
  104.8 6.5 %collective-permute-start.21 = (f32[6,8,3,128]{3,2,1,0:T(4,128)S(1)}, f32[6,8,3,128]{3,2,1,0:T(4,128)S(1)}, u32[]{:S(2)}, u32[]{:S(2)}) collective-permute-start(f32[6,8,3,128]{3,2,1,0:T(4,128)S(1)} %get-tuple-element.52), channel_id=1, source_target_pairs={{1,0},{2,1},{3,2},{4,3},{5,4},{6,5},{7,6},{9,8},{10,9},{11,10},{12... | collective-permute-start | bytes 221192 | tf_op jit(solution)/shard_map/ppermute | solution.py:48
  111.4 8.2 %collective-permute-start.23 = (f32[6,3,22,128]{3,2,1,0:T(8,128)S(1)}, f32[6,3,22,128]{3,2,1,0:T(8,128)S(1)}, u32[]{:S(2)}, u32[]{:S(2)}) collective-permute-start(f32[6,3,22,128]{3,2,1,0:T(8,128)S(1)} %pad_maximum_fusion.9), channel_id=1, source_target_pairs={{8,0},{16,8},{24,16},{9,1},{17,9},{25,17},{10,2},{18,10},{26,18},{... | collective-permute-start | bytes 608264 | tf_op jit(solution)/shard_map/ppermute | solution.py:48
  112.8 7.9 %collective-permute-start.22 = (f32[6,3,22,128]{3,2,1,0:T(8,128)S(1)}, f32[6,3,22,128]{3,2,1,0:T(8,128)S(1)}, u32[]{:S(2)}, u32[]{:S(2)}) collective-permute-start(f32[6,3,22,128]{3,2,1,0:T(8,128)S(1)} %pad_maximum_fusion.8), channel_id=1, source_target_pairs={{0,8},{8,16},{16,24},{1,9},{9,17},{17,25},{2,10},{10,18},{18,26},{... | collective-permute-start | bytes 608264 | tf_op jit(solution)/shard_map/ppermute | solution.py:48
  124.8 5.6 %collective-permute-start.24 = (f32[6,8,3,128]{3,2,1,0:T(4,128)S(1)}, f32[6,8,3,128]{3,2,1,0:T(4,128)S(1)}, u32[]{:S(2)}, u32[]{:S(2)}) collective-permute-start(f32[6,8,3,128]{3,2,1,0:T(4,128)S(1)} %get-tuple-element.49), channel_id=1, source_target_pairs={{0,1},{1,2},{2,3},{3,4},{4,5},{5,6},{6,7},{8,9},{9,10},{10,11},{11... | collective-permute-start | bytes 221192 | tf_op jit(solution)/shard_map/ppermute | solution.py:48
  128.2 6.5 %collective-permute-start.25 = (f32[6,8,3,128]{3,2,1,0:T(4,128)S(1)}, f32[6,8,3,128]{3,2,1,0:T(4,128)S(1)}, u32[]{:S(2)}, u32[]{:S(2)}) collective-permute-start(f32[6,8,3,128]{3,2,1,0:T(4,128)S(1)} %get-tuple-element.48), channel_id=1, source_target_pairs={{1,0},{2,1},{3,2},{4,3},{5,4},{6,5},{7,6},{9,8},{10,9},{11,10},{12... | collective-permute-start | bytes 221192 | tf_op jit(solution)/shard_map/ppermute | solution.py:48
  134.8 8.2 %collective-permute-start.27 = (f32[6,3,22,128]{3,2,1,0:T(8,128)S(1)}, f32[6,3,22,128]{3,2,1,0:T(8,128)S(1)}, u32[]{:S(2)}, u32[]{:S(2)}) collective-permute-start(f32[6,3,22,128]{3,2,1,0:T(8,128)S(1)} %pad_maximum_fusion.11), channel_id=1, source_target_pairs={{8,0},{16,8},{24,16},{9,1},{17,9},{25,17},{10,2},{18,10},{26,18},{... | collective-permute-start | bytes 608264 | tf_op jit(solution)/shard_map/ppermute | solution.py:48
  136.1 7.9 %collective-permute-start.26 = (f32[6,3,22,128]{3,2,1,0:T(8,128)S(1)}, f32[6,3,22,128]{3,2,1,0:T(8,128)S(1)}, u32[]{:S(2)}, u32[]{:S(2)}) collective-permute-start(f32[6,3,22,128]{3,2,1,0:T(8,128)S(1)} %pad_maximum_fusion.10), channel_id=1, source_target_pairs={{0,8},{8,16},{16,24},{1,9},{9,17},{17,25},{2,10},{10,18},{18,26},{... | collective-permute-start | bytes 608264 | tf_op jit(solution)/shard_map/ppermute | solution.py:48
  148.2 6.6 %collective-permute-start.28 = (f32[6,8,3,128]{3,2,1,0:T(4,128)S(1)}, f32[6,8,3,128]{3,2,1,0:T(4,128)S(1)}, u32[]{:S(2)}, u32[]{:S(2)}) collective-permute-start(f32[6,8,3,128]{3,2,1,0:T(4,128)S(1)} %get-tuple-element.45), channel_id=1, source_target_pairs={{0,1},{1,2},{2,3},{3,4},{4,5},{5,6},{6,7},{8,9},{9,10},{10,11},{11... | collective-permute-start | bytes 221192 | tf_op jit(solution)/shard_map/ppermute | solution.py:48
  152.6 6.5 %collective-permute-start.29 = (f32[6,8,3,128]{3,2,1,0:T(4,128)S(1)}, f32[6,8,3,128]{3,2,1,0:T(4,128)S(1)}, u32[]{:S(2)}, u32[]{:S(2)}) collective-permute-start(f32[6,8,3,128]{3,2,1,0:T(4,128)S(1)} %get-tuple-element.44), channel_id=1, source_target_pairs={{1,0},{2,1},{3,2},{4,3},{5,4},{6,5},{7,6},{9,8},{10,9},{11,10},{12... | collective-permute-start | bytes 221192 | tf_op jit(solution)/shard_map/ppermute | solution.py:48
  159.1 8.2 %collective-permute-start.31 = (f32[6,3,22,128]{3,2,1,0:T(8,128)S(1)}, f32[6,3,22,128]{3,2,1,0:T(8,128)S(1)}, u32[]{:S(2)}, u32[]{:S(2)}) collective-permute-start(f32[6,3,22,128]{3,2,1,0:T(8,128)S(1)} %pad_maximum_fusion.13), channel_id=1, source_target_pairs={{8,0},{16,8},{24,16},{9,1},{17,9},{25,17},{10,2},{18,10},{26,18},{... | collective-permute-start | bytes 608264 | tf_op jit(solution)/shard_map/ppermute | solution.py:48
  160.5 7.9 %collective-permute-start.30 = (f32[6,3,22,128]{3,2,1,0:T(8,128)S(1)}, f32[6,3,22,128]{3,2,1,0:T(8,128)S(1)}, u32[]{:S(2)}, u32[]{:S(2)}) collective-permute-start(f32[6,3,22,128]{3,2,1,0:T(8,128)S(1)} %pad_maximum_fusion.12), channel_id=1, source_target_pairs={{0,8},{8,16},{16,24},{1,9},{9,17},{17,25},{2,10},{10,18},{18,26},{... | collective-permute-start | bytes 608264 | tf_op jit(solution)/shard_map/ppermute | solution.py:48
  175.7 6.0 %collective-permute-start.33 = (f32[3,8,3,128]{3,2,1,0:T(4,128)S(1)}, f32[3,8,3,128]{3,2,1,0:T(4,128)S(1)}, u32[]{:S(2)}, u32[]{:S(2)}) collective-permute-start(f32[3,8,3,128]{3,2,1,0:T(4,128)S(1)} %get-tuple-element.40), channel_id=1, source_target_pairs={{1,0},{2,1},{3,2},{4,3},{5,4},{6,5},{7,6},{9,8},{10,9},{11,10},{12... | collective-permute-start | bytes 110600 | tf_op jit(solution)/shard_map/ppermute | solution.py:48
  181.7 8.2 %collective-permute-start.35 = (f32[3,3,22,128]{3,2,1,0:T(8,128)S(1)}, f32[3,3,22,128]{3,2,1,0:T(8,128)S(1)}, u32[]{:S(2)}, u32[]{:S(2)}) collective-permute-start(f32[3,3,22,128]{3,2,1,0:T(8,128)S(1)} %pad_maximum_fusion.15), channel_id=1, source_target_pairs={{8,0},{16,8},{24,16},{9,1},{17,9},{25,17},{10,2},{18,10},{26,18},{... | collective-permute-start | bytes 304136 | tf_op jit(solution)/shard_map/ppermute | solution.py:48
  183.1 7.7 %collective-permute-start.34 = (f32[3,3,22,128]{3,2,1,0:T(8,128)S(1)}, f32[3,3,22,128]{3,2,1,0:T(8,128)S(1)}, u32[]{:S(2)}, u32[]{:S(2)}) collective-permute-start(f32[3,3,22,128]{3,2,1,0:T(8,128)S(1)} %pad_maximum_fusion.14), channel_id=1, source_target_pairs={{0,8},{8,16},{16,24},{1,9},{9,17},{17,25},{2,10},{10,18},{18,26},{... | collective-permute-start | bytes 304136 | tf_op jit(solution)/shard_map/ppermute | solution.py:48
  (14 other events, 64.0 us)

commit v2 on v1

--- a/solution.py
+++ b/solution.py
@@ -20,7 +20,7 @@
         for b in range(-3, 4):
             for c in range(-3, 4):
                 if 0 < a * a + b * b + c * c <= 9:
-                    table.append((a, b, c))
+                    table.append((b, a, c))
     return table
 
 
@@ -39,40 +39,37 @@
     return 1.0 / (length * math.sqrt(length) * MASS)
 
 
-def shifted(x, axis, up):
-    ends = lax.axis_size(axis) - 1
-    if up:
-        pairs = [(i, i + 1) for i in range(ends)]
-    else:
-        pairs = [(i + 1, i) for i in range(ends)]
-    return lax.ppermute(x, axis, pairs)
-
-
 def halos(q, outside=None):
-    rows, cols = q.shape[1], q.shape[2]
-
-    def edge(lo, hi, axis):
-        if outside is None:
-            return lo, hi
-        at = lax.axis_index(axis)
-        lo = jnp.where(at == 0, outside, lo)
-        hi = jnp.where(at == lax.axis_size(axis) - 1, outside, hi)
-        return lo, hi
-
-    yl = shifted(q[:, :, cols - 3 :], "gy", True)
-    yr = shifted(q[:, :, :3], "gy", False)
-    yl, yr = edge(yl, yr, "gy")
-
-    def strip(part):
-        return jnp.concatenate([yl[:, part], q[:, part], yr[:, part]], axis=2)
-
-    xl = shifted(strip(slice(rows - 3, rows)), "gx", True)
-    xr = shifted(strip(slice(0, 3)), "gx", False)
-    xl, xr = edge(xl, xr, "gx")
-    return yl, yr, xl, xr
-
-
-def fill(ext, q, yl, yr, xl, xr, shift):
+    rows = q.shape[1]
+    across, along = lax.axis_size("gx"), lax.axis_size("gy")
+    slabs = [x * along + y for y in range(along) for x in range(across)]
+    at = lax.axis_index("gy") * across + lax.axis_index("gx")
+    lo, hi = [], []
+    hops = -(-3 // rows)
+    for hop in range(1, hops + 1):
+        need = min(rows, 3 - (hop - 1) * rows)
+        up = list(zip(slabs[:-hop], slabs[hop:]))
+        below = lax.ppermute(q[:, rows - need :], ("gx", "gy"), up)
+        above = lax.ppermute(q[:, :need], ("gx", "gy"), [(b, a) for a, b in up])
+        if outside is not None:
+            below = jnp.where(at < hop, outside, below)
+            above = jnp.where(at >= len(slabs) - hop, outside, above)
+        lo.insert(0, below)
+        hi.append(above)
+    if hops == 1:
+        return lo[0], hi[0]
+    return jnp.concatenate(lo, axis=1), jnp.concatenate(hi, axis=1)
+
+
+def to_slabs(x):
+    return lax.all_to_all(jnp.swapaxes(x, 1, 2), "gx", 1, 2, tiled=True)
+
+
+def from_slabs(x):
+    return jnp.swapaxes(lax.all_to_all(x, "gx", 2, 1, tiled=True), 1, 2)
+
+
+def fill(ext, q, lo, hi, shift):
     fields, rows, cols, depth = q.shape
     for f in range(fields):
         base = q[f, 0, 0:1, 0:1] if shift else None
@@ -81,10 +78,8 @@
             return x - base if shift else x
 
         ext[f, 3 : 3 + rows, LEAD : LEAD + cols, :] = moved(q[f])
-        ext[f, 3 : 3 + rows, LEAD - 3 : LEAD, :] = moved(yl[f])
-        ext[f, 3 : 3 + rows, LEAD + cols : LEAD + cols + 3, :] = moved(yr[f])
-        ext[f, 0:3, LEAD - 3 : LEAD + cols + 3, :] = moved(xl[f])
-        ext[f, 3 + rows :, LEAD - 3 : LEAD + cols + 3, :] = moved(xr[f])
+        ext[f, 0:3, LEAD : LEAD + cols, :] = moved(lo[f])
+        ext[f, 3 + rows :, LEAD : LEAD + cols, :] = moved(hi[f])
 
 
 def turn(x, by):
@@ -92,9 +87,10 @@
     return pltpu.roll(x, by % depth, x.ndim - 1)
 
 
-def prep_kernel(q, yl, yr, xl, xr, words_out, k_out, ext):
+def prep_kernel(q, lo, hi, words_out, k_out, ext):
     _, rows, cols, depth = q.shape
-    fill(ext, q, yl, yr, xl, xr, False)
+    ext[...] = jnp.full_like(ext, -1)
+    fill(ext, q, lo, hi, False)
 
     def row(r, carry):
         lane = lax.broadcasted_iota(jnp.int32, (8, depth), 1)
@@ -225,12 +221,12 @@
 
 
 def apply_kernel(kind, *refs):
-    q, yl, yr, xl, xr, words, k = refs[:7]
-    extra = refs[7:-3]
+    q, lo, hi, words, k = refs[:5]
+    extra = refs[5:-3]
     q_out, sums, ext = refs[-3:]
     fields, rows, cols, depth = q.shape
     chains = fields // 3
-    fill(ext, q, yl, yr, xl, xr, True)
+    fill(ext, q, lo, hi, True)
     sums[...] = jnp.zeros_like(sums)
 
     def row(r, carry):
@@ -239,10 +235,8 @@
             out = forces(ext, words, k, r, tile, chains)
             was = [[q[3 * ch + i, r, at, :] for i in range(3)] for ch in range(chains)]
             if kind == "first":
-                load, flags = extra
-                on = flags[r, at, :].astype(jnp.float32) * (1.0 / MASS)
                 for i in range(3):
-                    out[0][i] = out[0][i] + on * load[i, r, at, :]
+                    out[0][i] = out[0][i] + extra[0][i, r, at, :] * (1.0 / MASS)
             for ch in range(chains):
                 for i in range(3):
                     q_out[3 * ch + i, r, at, :] = out[ch][i]
@@ -296,10 +290,10 @@
 
 
 def finish_kernel(count, rounds, *refs):
-    m, disp, vel = refs[:3]
-    qs = refs[3 : 3 + rounds]
-    u_out, v_out = refs[-2:]
-    rows, cols, depth = disp.shape[1:]
+    m, start = refs[:2]
+    qs = refs[2 : 2 + rounds]
+    out = refs[-1]
+    rows, cols, depth = start.shape[1:]
 
     def moment(step, which):
         at = 6 * step + which
@@ -343,14 +337,14 @@
         for tile in range(cols // 8):
             at = pl.ds(tile * 8, 8)
             for i in range(3):
-                u, v = disp[i, at_row, at, :], None
+                u, v = start[i, at_row, at, :], None
                 for j in range(rounds):
-                    x = vel[i, at_row, at, :] if j == 0 else qs[j - 1][3 + i, at_row, at, :]
+                    x = start[3 + i, at_row, at, :] if j == 0 else qs[j - 1][3 + i, at_row, at, :]
                     y = qs[j][i, at_row, at, :]
                     u = u + up[j] * x + uq[j] * y
                     v = plus(v, p[j] * x + q[j] * y)
-                u_out[i, at_row, at, :] = u
-                v_out[i, at_row, at, :] = v
+                out[i, at_row, at, :] = u
+                out[3 + i, at_row, at, :] = v
         return carry
 
     lax.fori_loop(0, rows, row, 0)
@@ -373,6 +367,12 @@
     _, rows, cols, depth = disp.shape
     count = 3.0 * rows * lax.axis_size("gx") * cols * lax.axis_size("gy") * depth
     f32, i32 = jnp.float32, jnp.int32
+    applied = flags.astype(f32)[None] * load
+    parts = [x[i : i + 1] for x in (disp, vel, applied) for i in (1, 0, 2)]
+    fields = to_slabs(jnp.concatenate(parts))
+    masks = to_slabs(mask_bits)
+    start, applied = fields[:6], fields[6:]
+    _, rows, cols, depth = start.shape
 
     def scratch(fields, kind):
         return [pltpu.VMEM((fields, rows + 6, cols + 2 * LEAD, depth), kind)]
@@ -386,7 +386,7 @@
         scratch_shapes=scratch(4, i32),
         compiler_params=VMEM,
         name="prep",
-    )(mask_bits, *halos(mask_bits, -1))
+    )(masks, *halos(masks, -1))
 
     def applied_to(q, kind, *extra):
         fields = q.shape[0]
@@ -405,7 +405,7 @@
             name="apply_" + kind,
         )(q, *halos(q), words, k, *extra)
 
-    q, sums = applied_to(jnp.concatenate([disp, vel]), "first", load, flags)
+    q, sums = applied_to(start, "first", applied)
     qs, parts = [q], [sums]
     for step in range(1, ITERS - 1):
         q, sums = applied_to(q, "mid")
@@ -421,12 +421,15 @@
     def body(*refs):
         finish_kernel(count, ITERS, *refs)
 
-    return pl.pallas_call(
+    done = pl.pallas_call(
         body,
-        out_shape=(jax.ShapeDtypeStruct(disp.shape, f32), jax.ShapeDtypeStruct(vel.shape, f32)),
+        out_shape=jax.ShapeDtypeStruct(start.shape, f32),
         compiler_params=VMEM,
         name="finish",
-    )(spread, disp, vel, *qs)
+    )(spread, start, *qs)
+    done = from_slabs(done)
+    u, v = ([done[base + i] for i in (1, 0, 2)] for base in (0, 3))
+    return jnp.stack(u), jnp.stack(v)
 
 
 def solution(mesh):

time: 218 us -> 182 us (0.83)
  waiting for transfers between devices: 56.7 us -> 28 us
  starting transfers between devices: 118 us -> 94.9 us
  blocking collectives: 0 us -> 10.5 us
  local copies, waits for them, and re-layouts: 1.99 us -> 9.96 us
    ppermute x36 -> x18, starting transfers between devices: 110 us -> 69 us  [the longest x9 57.4 us: halos(): below = lax.ppermute(q[:, rows - need:], ('gx', 'gy'), up)]
    ppermute x36 -> x18, waiting for transfers between devices: 43.6 us -> 14.9 us  [the longest x9 14.9 us: halos(): above = lax.ppermute(q[:, :need], ('gx', 'gy'), [(b, a) for a, b in up])]
    all_to_all x0 -> x1, blocking collectives: none -> 10.5 us  [from_slabs(): return jnp.swapaxes(lax.all_to_all(x, 'gx', 2, 1, tiled=True), 1, 2)]
    ppermute x5, starting transfers between devices: 8.33 us -> 18 us  [summed(): x = x + lax.ppermute(x, axis, [(i, i ^ step) for i in range(size)])]
    unnamed x18 -> x24, local copies, waits for them, and re-layouts: 0.08 us -> 8.14 us
    all_to_all x0 -> x2, starting transfers between devices: none -> 7.87 us  [to_slabs(): return lax.all_to_all(jnp.swapaxes(x, 1, 2), 'gx', 1, 2, tiled=True)]
    all_to_all x0 -> x2, waiting for transfers between devices: none -> 5.34 us  [to_slabs(): return lax.all_to_all(jnp.swapaxes(x, 1, 2), 'gx', 1, 2, tiled=True)]
    ppermute x5, waiting for transfers between devices: 13.1 us -> 7.78 us  [summed(): x = x + lax.ppermute(x, axis, [(i, i ^ step) for i in range(size)])]
  transfers between devices with their start and end apart: 41 -> 25, of which waited for: 26 -> 13; matrix products, arithmetic and copies ran while one was open for 0% -> 3% of each run, Pallas kernels for 2% -> 2%
where the time goes in v2:
time: 182 us; the launch traced here: 181 us
  starting transfers between devices  94.9 us (52%)
  Pallas kernels  35.8 us (20%)
  waiting for transfers between devices  28 us (15%)
  blocking collectives  10.5 us (6%)
  local copies, waits for them, and re-layouts  9.96 us (5%)
    ppermute x9, starting transfers between devices, halos(): below = lax.ppermute(q[:, rows - need:], ('gx', 'gy'), up)  57.4 us
    pallas_call x8, Pallas kernels, applied_to(): pl.pallas_call(body, out_shape=(jax.ShapeDtypeStruct(q.shape, f32), jax.S...  30.4 us
    ppermute x5, starting transfers between devices, summed(): x = x + lax.ppermute(x, axis, [(i, i ^ step) for i in range(size)])  18 us
    ppermute x9, waiting for transfers between devices, halos(): above = lax.ppermute(q[:, :need], ('gx', 'gy'), [(b, a) for a, b in up])  14.9 us
    ppermute x9, starting transfers between devices, halos(): above = lax.ppermute(q[:, :need], ('gx', 'gy'), [(b, a) for a, b in up])  11.6 us
    all_to_all x1, blocking collectives, from_slabs(): return jnp.swapaxes(lax.all_to_all(x, 'gx', 2, 1, tiled=True), 1, 2)  10.5 us
    unnamed x24, local copies, waits for them, and re-layouts  8.14 us
    all_to_all x2, starting transfers between devices, to_slabs(): return lax.all_to_all(jnp.swapaxes(x, 1, 2), 'gx', 1, 2, tiled=True)  7.87 us
  transfers between devices with their start and end apart: 25, of which 13 were waited for; matrix products, arithmetic and copies ran while one was open for 3% of the time, Pallas kernels for 2%

profile of v2, /device:TPU:0, one launch (start us, length us, event | category | flops | bytes accessed | tf_op | source)
XLA Modules:
  0.0 181.4 jit_solution(7153937658653728441)
XLA Ops:
  2.4 4.4 %all-to-all-start.1 = ((s32[4,16,8,128]{3,2,0,1:T(8,128)}), s32[4,16,8,128]{3,2,0,1:T(8,128)S(1)}, u32[]{:S(2)}, u32[]{:S(2)}) async-start(s32[4,16,8,128]{3,2,0,1:T(8,128)} %bitcast.45), calls=%async_computation.1 | async-start | bytes 524288 | tf_op jit(solution)/shard_map/all_to_all | solution.py:65
  13.9 3.5 %all-to-all-start = ((f32[9,16,8,128]{3,2,0,1:T(8,128)}), f32[9,16,8,128]{3,2,0,1:T(8,128)S(1)}, u32[]{:S(2)}, u32[]{:S(2)}) async-start(f32[9,16,8,128]{3,2,0,1:T(8,128)} %bitcast), calls=%async_computation | async-start | bytes 1179648 | tf_op jit(solution)/shard_map/all_to_all | solution.py:65
  18.8 3.0 %collective-permute-start.2 = (s32[4,3,32,128]{3,2,1,0:T(8,128)S(1)}, s32[4,3,32,128]{3,2,1,0:T(8,128)S(1)}, u32[]{:S(2)}, u32[]{:S(2)}) collective-permute-start(s32[4,3,32,128]{3,2,1,0:T(8,128)S(1)} %get-tuple-element.61), channel_id=1, source_target_pairs={{0,8},{8,16},{16,24},{24,1},{1,9},{9,17},{17,25},{25,2},{2,10},{10... | collective-permute-start | bytes 589832 | tf_op jit(solution)/shard_map/ppermute | solution.py:52
  21.9 5.3 %all-to-all-done = f32[9,16,8,128]{3,2,0,1:T(8,128)S(1)} async-done(((f32[9,16,8,128]{3,2,0,1:T(8,128)}), f32[9,16,8,128]{3,2,0,1:T(8,128)S(1)}, u32[]{:S(2)}, u32[]{:S(2)}) %all-to-all-start) | async-done | bytes 589856 | tf_op jit(solution)/shard_map/all_to_all | solution.py:65
  27.4 3.6 %collective-permute-start = (f32[6,3,32,128]{3,2,1,0:T(8,128)S(1)}, f32[6,3,32,128]{3,2,1,0:T(8,128)S(1)}, u32[]{:S(2)}, u32[]{:S(2)}) collective-permute-start(f32[6,3,32,128]{3,2,1,0:T(8,128)S(1)} %get-tuple-element.59), channel_id=1, source_target_pairs={{0,8},{8,16},{16,24},{24,1},{1,9},{9,17},{17,25},{25,2},{2,10},{10... | collective-permute-start | bytes 884744 | tf_op jit(solution)/shard_map/ppermute | solution.py:52
  32.3 4.5 %prep.1 = (s32[5,4,32,128]{3,2,1,0:T(8,128)S(1)}, f32[6,4,32,128]{3,2,1,0:T(8,128)S(1)}) custom-call(s32[4,4,32,128]{3,2,1,0:T(8,128)S(1)} %bitcast.47, s32[4,3,32,128]{3,2,1,0:T(8,128)S(1)} %broadcast_select_fusion.1.lo, s32[4,3,32,128]{3,2,1,0:T(8,128)S(1)} %broadcast_select_fusion.hi), custom_call_target="tpu_custom_call" | custom-call | tf_op jit(solution)/shard_map/prep/pallas_call | solution.py:380
  36.8 4.0 %apply_first.1 = (f32[6,4,32,128]{3,2,1,0:T(8,128)S(1)}, f32[6,8,128]{2,1,0:T(8,128)S(1)}) custom-call(f32[6,4,32,128]{3,2,1,0:T(8,128)S(1)} %slice_bitcast_fusion.refs_0_.refs_1_, f32[6,3,32,128]{3,2,1,0:T(8,128)S(1)} %collective-permute-done.refs_1_, f32[6,3,32,128]{3,2,1,0:T(8,128)S(1)} %collective-permute-done.1.refs_2_, ...), custom_call_target="tpu_custom_call" | custom-call | tf_op jit(solution)/shard_map/apply_first/pallas_call | solution.py:397
  40.9 4.9 %collective-permute-start.4 = (f32[6,3,32,128]{3,2,1,0:T(8,128)S(1)}, f32[6,3,32,128]{3,2,1,0:T(8,128)S(1)}, u32[]{:S(2)}, u32[]{:S(2)}) collective-permute-start(f32[6,3,32,128]{3,2,1,0:T(8,128)S(1)} %get-tuple-element.57), channel_id=1, source_target_pairs={{0,8},{8,16},{16,24},{24,1},{1,9},{9,17},{17,25},{25,2},{2,10},{10... | collective-permute-start | bytes 884744 | tf_op jit(solution)/shard_map/ppermute | solution.py:52
  47.2 2.2 %collective-permute-done.5.refs_2_ = f32[6,3,32,128]{3,2,1,0:T(8,128)S(1)} collective-permute-done((f32[6,3,32,128]{3,2,1,0:T(8,128)S(1)}, f32[6,3,32,128]{3,2,1,0:T(8,128)S(1)}, u32[]{:S(2)}, u32[]{:S(2)}) %collective-permute-start.5) | collective-permute-done | bytes 294944 | tf_op jit(solution)/shard_map/ppermute | solution.py:53
  49.3 4.0 %apply_mid.6 = (f32[6,4,32,128]{3,2,1,0:T(8,128)S(1)}, f32[6,8,128]{2,1,0:T(8,128)S(1)}) custom-call(f32[6,4,32,128]{3,2,1,0:T(8,128)S(1)} %get-tuple-element.23.refs_0_.refs_2_, f32[6,3,32,128]{3,2,1,0:T(8,128)S(1)} %collective-permute-done.4.refs_1_, f32[6,3,32,128]{3,2,1,0:T(8,128)S(1)} %collective-permute-done.5.refs_2_, ...), custom_call_target="tpu_custom_call" | custom-call | tf_op jit(solution)/shard_map/apply_mid/pallas_call | solution.py:397
  53.4 8.7 %collective-permute-start.6 = (f32[6,3,32,128]{3,2,1,0:T(8,128)S(1)}, f32[6,3,32,128]{3,2,1,0:T(8,128)S(1)}, u32[]{:S(2)}, u32[]{:S(2)}) collective-permute-start(f32[6,3,32,128]{3,2,1,0:T(8,128)S(1)} %get-tuple-element.55), channel_id=1, source_target_pairs={{0,8},{8,16},{16,24},{24,1},{1,9},{9,17},{17,25},{25,2},{2,10},{10... | collective-permute-start | bytes 884744 | tf_op jit(solution)/shard_map/ppermute | solution.py:52
  63.5 2.2 %collective-permute-done.7.refs_2_ = f32[6,3,32,128]{3,2,1,0:T(8,128)S(1)} collective-permute-done((f32[6,3,32,128]{3,2,1,0:T(8,128)S(1)}, f32[6,3,32,128]{3,2,1,0:T(8,128)S(1)}, u32[]{:S(2)}, u32[]{:S(2)}) %collective-permute-start.7) | collective-permute-done | bytes 294944 | tf_op jit(solution)/shard_map/ppermute | solution.py:53
  65.7 4.0 %apply_mid.7 = (f32[6,4,32,128]{3,2,1,0:T(8,128)S(1)}, f32[6,8,128]{2,1,0:T(8,128)S(1)}) custom-call(f32[6,4,32,128]{3,2,1,0:T(8,128)S(1)} %get-tuple-element.25.refs_0_.refs_3_, f32[6,3,32,128]{3,2,1,0:T(8,128)S(1)} %collective-permute-done.6.refs_1_, f32[6,3,32,128]{3,2,1,0:T(8,128)S(1)} %collective-permute-done.7.refs_2_, ...), custom_call_target="tpu_custom_call" | custom-call | tf_op jit(solution)/shard_map/apply_mid/pallas_call | solution.py:397
  69.8 7.6 %collective-permute-start.8 = (f32[6,3,32,128]{3,2,1,0:T(8,128)S(1)}, f32[6,3,32,128]{3,2,1,0:T(8,128)S(1)}, u32[]{:S(2)}, u32[]{:S(2)}) collective-permute-start(f32[6,3,32,128]{3,2,1,0:T(8,128)S(1)} %get-tuple-element.53), channel_id=1, source_target_pairs={{0,8},{8,16},{16,24},{24,1},{1,9},{9,17},{17,25},{25,2},{2,10},{10... | collective-permute-start | bytes 884744 | tf_op jit(solution)/shard_map/ppermute | solution.py:52
  78.7 2.2 %collective-permute-done.9.refs_2_ = f32[6,3,32,128]{3,2,1,0:T(8,128)S(1)} collective-permute-done((f32[6,3,32,128]{3,2,1,0:T(8,128)S(1)}, f32[6,3,32,128]{3,2,1,0:T(8,128)S(1)}, u32[]{:S(2)}, u32[]{:S(2)}) %collective-permute-start.9) | collective-permute-done | bytes 294944 | tf_op jit(solution)/shard_map/ppermute | solution.py:53
  80.8 4.0 %apply_mid.8 = (f32[6,4,32,128]{3,2,1,0:T(8,128)S(1)}, f32[6,8,128]{2,1,0:T(8,128)S(1)}) custom-call(f32[6,4,32,128]{3,2,1,0:T(8,128)S(1)} %get-tuple-element.27.refs_0_.refs_4_, f32[6,3,32,128]{3,2,1,0:T(8,128)S(1)} %collective-permute-done.8.refs_1_, f32[6,3,32,128]{3,2,1,0:T(8,128)S(1)} %collective-permute-done.9.refs_2_, ...), custom_call_target="tpu_custom_call" | custom-call | tf_op jit(solution)/shard_map/apply_mid/pallas_call | solution.py:397
  84.9 7.4 %collective-permute-start.10 = (f32[6,3,32,128]{3,2,1,0:T(8,128)S(1)}, f32[6,3,32,128]{3,2,1,0:T(8,128)S(1)}, u32[]{:S(2)}, u32[]{:S(2)}) collective-permute-start(f32[6,3,32,128]{3,2,1,0:T(8,128)S(1)} %get-tuple-element.51), channel_id=1, source_target_pairs={{0,8},{8,16},{16,24},{24,1},{1,9},{9,17},{17,25},{25,2},{2,10},{10... | collective-permute-start | bytes 884744 | tf_op jit(solution)/shard_map/ppermute | solution.py:52
  93.7 2.1 %collective-permute-done.11.refs_2_ = f32[6,3,32,128]{3,2,1,0:T(8,128)S(1)} collective-permute-done((f32[6,3,32,128]{3,2,1,0:T(8,128)S(1)}, f32[6,3,32,128]{3,2,1,0:T(8,128)S(1)}, u32[]{:S(2)}, u32[]{:S(2)}) %collective-permute-start.11) | collective-permute-done | bytes 294944 | tf_op jit(solution)/shard_map/ppermute | solution.py:53
  95.8 4.0 %apply_mid.9 = (f32[6,4,32,128]{3,2,1,0:T(8,128)S(1)}, f32[6,8,128]{2,1,0:T(8,128)S(1)}) custom-call(f32[6,4,32,128]{3,2,1,0:T(8,128)S(1)} %get-tuple-element.29.refs_0_.refs_5_, f32[6,3,32,128]{3,2,1,0:T(8,128)S(1)} %collective-permute-done.10.refs_1_, f32[6,3,32,128]{3,2,1,0:T(8,128)S(1)} %collective-permute-done.11.refs_2_, ...), custom_call_target="tpu_custom_call" | custom-call | tf_op jit(solution)/shard_map/apply_mid/pallas_call | solution.py:397
  99.9 7.4 %collective-permute-start.12 = (f32[6,3,32,128]{3,2,1,0:T(8,128)S(1)}, f32[6,3,32,128]{3,2,1,0:T(8,128)S(1)}, u32[]{:S(2)}, u32[]{:S(2)}) collective-permute-start(f32[6,3,32,128]{3,2,1,0:T(8,128)S(1)} %get-tuple-element.49), channel_id=1, source_target_pairs={{0,8},{8,16},{16,24},{24,1},{1,9},{9,17},{17,25},{25,2},{2,10},{10... | collective-permute-start | bytes 884744 | tf_op jit(solution)/shard_map/ppermute | solution.py:52
  108.7 2.1 %collective-permute-done.13.refs_2_ = f32[6,3,32,128]{3,2,1,0:T(8,128)S(1)} collective-permute-done((f32[6,3,32,128]{3,2,1,0:T(8,128)S(1)}, f32[6,3,32,128]{3,2,1,0:T(8,128)S(1)}, u32[]{:S(2)}, u32[]{:S(2)}) %collective-permute-start.13) | collective-permute-done | bytes 294944 | tf_op jit(solution)/shard_map/ppermute | solution.py:53
  110.8 4.0 %apply_mid.10 = (f32[6,4,32,128]{3,2,1,0:T(8,128)S(1)}, f32[6,8,128]{2,1,0:T(8,128)S(1)}) custom-call(f32[6,4,32,128]{3,2,1,0:T(8,128)S(1)} %get-tuple-element.31.refs_0_.refs_6_, f32[6,3,32,128]{3,2,1,0:T(8,128)S(1)} %collective-permute-done.12.refs_1_, f32[6,3,32,128]{3,2,1,0:T(8,128)S(1)} %collective-permute-done.13.refs_2_, ...), custom_call_target="tpu_custom_call" | custom-call | tf_op jit(solution)/shard_map/apply_mid/pallas_call | solution.py:397
  114.9 7.4 %collective-permute-start.14 = (f32[6,3,32,128]{3,2,1,0:T(8,128)S(1)}, f32[6,3,32,128]{3,2,1,0:T(8,128)S(1)}, u32[]{:S(2)}, u32[]{:S(2)}) collective-permute-start(f32[6,3,32,128]{3,2,1,0:T(8,128)S(1)} %get-tuple-element.47), channel_id=1, source_target_pairs={{0,8},{8,16},{16,24},{24,1},{1,9},{9,17},{17,25},{25,2},{2,10},{10... | collective-permute-start | bytes 884744 | tf_op jit(solution)/shard_map/ppermute | solution.py:52
  123.6 2.1 %collective-permute-done.15.refs_2_ = f32[6,3,32,128]{3,2,1,0:T(8,128)S(1)} collective-permute-done((f32[6,3,32,128]{3,2,1,0:T(8,128)S(1)}, f32[6,3,32,128]{3,2,1,0:T(8,128)S(1)}, u32[]{:S(2)}, u32[]{:S(2)}) %collective-permute-start.15) | collective-permute-done | bytes 294944 | tf_op jit(solution)/shard_map/ppermute | solution.py:53
  125.8 4.0 %apply_mid.11 = (f32[6,4,32,128]{3,2,1,0:T(8,128)S(1)}, f32[6,8,128]{2,1,0:T(8,128)S(1)}) custom-call(f32[6,4,32,128]{3,2,1,0:T(8,128)S(1)} %get-tuple-element.33.refs_0_.refs_7_, f32[6,3,32,128]{3,2,1,0:T(8,128)S(1)} %collective-permute-done.14.refs_1_, f32[6,3,32,128]{3,2,1,0:T(8,128)S(1)} %collective-permute-done.15.refs_2_, ...), custom_call_target="tpu_custom_call" | custom-call | tf_op jit(solution)/shard_map/apply_mid/pallas_call | solution.py:397
  129.9 7.4 %collective-permute-start.16 = (f32[3,3,32,128]{3,2,1,0:T(8,128)S(1)}, f32[3,3,32,128]{3,2,1,0:T(8,128)S(1)}, u32[]{:S(2)}, u32[]{:S(2)}) collective-permute-start(f32[3,3,32,128]{3,2,1,0:T(8,128)S(1)} %get-tuple-element.45), channel_id=1, source_target_pairs={{0,8},{8,16},{16,24},{24,1},{1,9},{9,17},{17,25},{25,2},{2,10},{10... | collective-permute-start | bytes 442376 | tf_op jit(solution)/shard_map/ppermute | solution.py:52
  140.5 2.1 %apply_last.1 = (f32[3,4,32,128]{3,2,1,0:T(8,128)S(1)}, f32[6,8,128]{2,1,0:T(8,128)S(1)}) custom-call(f32[3,4,32,128]{3,2,1,0:T(8,128)S(1)} %slice.149.refs_0_, f32[3,3,32,128]{3,2,1,0:T(8,128)S(1)} %collective-permute-done.16.refs_1_, f32[3,3,32,128]{3,2,1,0:T(8,128)S(1)} %collective-permute-done.17.refs_2_, ...), custom_call_target="tpu_custom_call" | custom-call | tf_op jit(solution)/shard_map/apply_last/pallas_call | solution.py:397
  142.9 5.0 %collective-permute-start.18 = (f32[1,128]{1,0:T(1,128)S(1)}, f32[1,128]{1,0:T(1,128)S(1)}, u32[]{:S(2)}, u32[]{:S(2)}) collective-permute-start(f32[1,128]{1,0:T(1,128)S(1)} %pad_bitcast_fusion), channel_id=1, source_target_pairs={{0,8},{8,0},{16,24},{24,16},{1,9},{9,1},{17,25},{25,17},{2,10},{10... | collective-permute-start | bytes 1544 | tf_op jit(solution)/shard_map/ppermute | solution.py:361
  148.8 3.4 %collective-permute-start.19 = (f32[1,128]{1,0:T(1,128)S(1)}, f32[1,128]{1,0:T(1,128)S(1)}, u32[]{:S(2)}, u32[]{:S(2)}) collective-permute-start(f32[1,128]{1,0:T(1,128)S(1)} %fusion), channel_id=1, source_target_pairs={{0,16},{8,24},{16,0},{24,8},{1,17},{9,25},{17,1},{25,9},{2,18},{10... | collective-permute-start | bytes 1544 | tf_op jit(solution)/shard_map/ppermute | solution.py:361
  153.7 5.4 %collective-permute-start.20 = (f32[1,128]{1,0:T(1,128)S(1)}, f32[1,128]{1,0:T(1,128)S(1)}, u32[]{:S(2)}, u32[]{:S(2)}) collective-permute-start(f32[1,128]{1,0:T(1,128)S(1)} %add.22), channel_id=1, source_target_pairs={{0,1},{1,0},{2,3},{3,2},{4,5},{5,4},{6,7},{7,6},{8,9},{9,8},{10,11... | collective-permute-start | bytes 1544 | tf_op jit(solution)/shard_map/ppermute | solution.py:361
  164.3 2.6 %collective-permute-start.22 = (f32[1,128]{1,0:T(1,128)S(1)}, f32[1,128]{1,0:T(1,128)S(1)}, u32[]{:S(2)}, u32[]{:S(2)}) collective-permute-start(f32[1,128]{1,0:T(1,128)S(1)} %add.24), channel_id=1, source_target_pairs={{0,4},{1,5},{2,6},{3,7},{4,0},{5,1},{6,2},{7,3},{8,12},{9,13},{10,... | collective-permute-start | bytes 1544 | tf_op jit(solution)/shard_map/ppermute | solution.py:361
  170.0 10.5 %all_to_all.51 = f32[6,4,32,128]{3,1,0,2:T(4,128)S(1)} all-to-all(f32[6,4,32,128]{3,1,0,2:T(4,128)S(1)} %copy.21), channel_id=1, replica_groups=mesh['gx'=4,'gy'=8] {'gx'}, dimensions={2} | all-to-all | bytes 786432 | tf_op jit(solution)/shard_map/all_to_all | solution.py:69
  (90 shorter events, 34.9 us)
Async XLA Ops:
  2.4 4.4 %copy-start.1 = (f32[3,8,16,128]{3,2,1,0:T(8,128)S(1)}, f32[3,8,16,128]{3,2,1,0:T(8,128)}, u32[]{:S(2)}) copy-start(f32[3,8,16,128]{3,2,1,0:T(8,128)} %param.5) | copy-start | bytes 589828
  2.4 11.6 %all-to-all-start.1 = ((s32[4,16,8,128]{3,2,0,1:T(8,128)}), s32[4,16,8,128]{3,2,0,1:T(8,128)S(1)}, u32[]{:S(2)}, u32[]{:S(2)}) async-start(s32[4,16,8,128]{3,2,0,1:T(8,128)} %bitcast.45), calls=%async_computation.1 | async-start | bytes 524288 | tf_op jit(solution)/shard_map/all_to_all | solution.py:65
  6.8 1.0 copy-start.2
  7.7 0.8 copy-start.3
  9.9 2.0 %copy-start = (f32[3,8,16,128]{3,2,1,0:T(8,128)S(1)}, f32[3,8,16,128]{3,2,1,0:T(8,128)}, u32[]{:S(2)}) copy-start(f32[3,8,16,128]{3,2,1,0:T(8,128)} %param.7) | copy-start | bytes 589828
  13.9 13.3 %all-to-all-start = ((f32[9,16,8,128]{3,2,0,1:T(8,128)}), f32[9,16,8,128]{3,2,0,1:T(8,128)S(1)}, u32[]{:S(2)}, u32[]{:S(2)}) async-start(f32[9,16,8,128]{3,2,0,1:T(8,128)} %bitcast), calls=%async_computation | async-start | bytes 1179648 | tf_op jit(solution)/shard_map/all_to_all | solution.py:65
  17.5 4.4 %collective-permute-start.3 = (s32[4,3,32,128]{3,2,1,0:T(8,128)S(1)}, s32[4,3,32,128]{3,2,1,0:T(8,128)S(1)}, u32[]{:S(2)}, u32[]{:S(2)}) collective-permute-start(s32[4,3,32,128]{3,2,1,0:T(8,128)S(1)} %get-tuple-element.60), channel_id=1, source_target_pairs={{8,0},{16,8},{24,16},{1,24},{9,1},{17,9},{25,17},{2,25},{10,2},{18... | collective-permute-start | bytes 589832 | tf_op jit(solution)/shard_map/ppermute | solution.py:53
  18.8 13.5 %collective-permute-start.2 = (s32[4,3,32,128]{3,2,1,0:T(8,128)S(1)}, s32[4,3,32,128]{3,2,1,0:T(8,128)S(1)}, u32[]{:S(2)}, u32[]{:S(2)}) collective-permute-start(s32[4,3,32,128]{3,2,1,0:T(8,128)S(1)} %get-tuple-element.61), channel_id=1, source_target_pairs={{0,8},{8,16},{16,24},{24,1},{1,9},{9,17},{17,25},{25,2},{2,10},{10... | collective-permute-start | bytes 589832 | tf_op jit(solution)/shard_map/ppermute | solution.py:52
  27.4 9.4 %collective-permute-start = (f32[6,3,32,128]{3,2,1,0:T(8,128)S(1)}, f32[6,3,32,128]{3,2,1,0:T(8,128)S(1)}, u32[]{:S(2)}, u32[]{:S(2)}) collective-permute-start(f32[6,3,32,128]{3,2,1,0:T(8,128)S(1)} %get-tuple-element.59), channel_id=1, source_target_pairs={{0,8},{8,16},{16,24},{24,1},{1,9},{9,17},{17,25},{25,2},{2,10},{10... | collective-permute-start | bytes 884744 | tf_op jit(solution)/shard_map/ppermute | solution.py:52
  31.0 5.9 %collective-permute-start.1 = (f32[6,3,32,128]{3,2,1,0:T(8,128)S(1)}, f32[6,3,32,128]{3,2,1,0:T(8,128)S(1)}, u32[]{:S(2)}, u32[]{:S(2)}) collective-permute-start(f32[6,3,32,128]{3,2,1,0:T(8,128)S(1)} %get-tuple-element.58), channel_id=1, source_target_pairs={{8,0},{16,8},{24,16},{1,24},{9,1},{17,9},{25,17},{2,25},{10,2},{18... | collective-permute-start | bytes 884744 | tf_op jit(solution)/shard_map/ppermute | solution.py:53
  40.9 6.3 %collective-permute-start.4 = (f32[6,3,32,128]{3,2,1,0:T(8,128)S(1)}, f32[6,3,32,128]{3,2,1,0:T(8,128)S(1)}, u32[]{:S(2)}, u32[]{:S(2)}) collective-permute-start(f32[6,3,32,128]{3,2,1,0:T(8,128)S(1)} %get-tuple-element.57), channel_id=1, source_target_pairs={{0,8},{8,16},{16,24},{24,1},{1,9},{9,17},{17,25},{25,2},{2,10},{10... | collective-permute-start | bytes 884744 | tf_op jit(solution)/shard_map/ppermute | solution.py:52
  45.8 3.5 %collective-permute-start.5 = (f32[6,3,32,128]{3,2,1,0:T(8,128)S(1)}, f32[6,3,32,128]{3,2,1,0:T(8,128)S(1)}, u32[]{:S(2)}, u32[]{:S(2)}) collective-permute-start(f32[6,3,32,128]{3,2,1,0:T(8,128)S(1)} %get-tuple-element.56), channel_id=1, source_target_pairs={{8,0},{16,8},{24,16},{1,24},{9,1},{17,9},{25,17},{2,25},{10,2},{18... | collective-permute-start | bytes 884744 | tf_op jit(solution)/shard_map/ppermute | solution.py:53
  53.4 10.1 %collective-permute-start.6 = (f32[6,3,32,128]{3,2,1,0:T(8,128)S(1)}, f32[6,3,32,128]{3,2,1,0:T(8,128)S(1)}, u32[]{:S(2)}, u32[]{:S(2)}) collective-permute-start(f32[6,3,32,128]{3,2,1,0:T(8,128)S(1)} %get-tuple-element.55), channel_id=1, source_target_pairs={{0,8},{8,16},{16,24},{24,1},{1,9},{9,17},{17,25},{25,2},{2,10},{10... | collective-permute-start | bytes 884744 | tf_op jit(solution)/shard_map/ppermute | solution.py:52
  62.2 3.5 %collective-permute-start.7 = (f32[6,3,32,128]{3,2,1,0:T(8,128)S(1)}, f32[6,3,32,128]{3,2,1,0:T(8,128)S(1)}, u32[]{:S(2)}, u32[]{:S(2)}) collective-permute-start(f32[6,3,32,128]{3,2,1,0:T(8,128)S(1)} %get-tuple-element.54), channel_id=1, source_target_pairs={{8,0},{16,8},{24,16},{1,24},{9,1},{17,9},{25,17},{2,25},{10,2},{18... | collective-permute-start | bytes 884744 | tf_op jit(solution)/shard_map/ppermute | solution.py:53
  69.8 8.9 %collective-permute-start.8 = (f32[6,3,32,128]{3,2,1,0:T(8,128)S(1)}, f32[6,3,32,128]{3,2,1,0:T(8,128)S(1)}, u32[]{:S(2)}, u32[]{:S(2)}) collective-permute-start(f32[6,3,32,128]{3,2,1,0:T(8,128)S(1)} %get-tuple-element.53), channel_id=1, source_target_pairs={{0,8},{8,16},{16,24},{24,1},{1,9},{9,17},{17,25},{25,2},{2,10},{10... | collective-permute-start | bytes 884744 | tf_op jit(solution)/shard_map/ppermute | solution.py:52
  77.4 3.5 %collective-permute-start.9 = (f32[6,3,32,128]{3,2,1,0:T(8,128)S(1)}, f32[6,3,32,128]{3,2,1,0:T(8,128)S(1)}, u32[]{:S(2)}, u32[]{:S(2)}) collective-permute-start(f32[6,3,32,128]{3,2,1,0:T(8,128)S(1)} %get-tuple-element.52), channel_id=1, source_target_pairs={{8,0},{16,8},{24,16},{1,24},{9,1},{17,9},{25,17},{2,25},{10,2},{18... | collective-permute-start | bytes 884744 | tf_op jit(solution)/shard_map/ppermute | solution.py:53
  84.9 8.7 %collective-permute-start.10 = (f32[6,3,32,128]{3,2,1,0:T(8,128)S(1)}, f32[6,3,32,128]{3,2,1,0:T(8,128)S(1)}, u32[]{:S(2)}, u32[]{:S(2)}) collective-permute-start(f32[6,3,32,128]{3,2,1,0:T(8,128)S(1)} %get-tuple-element.51), channel_id=1, source_target_pairs={{0,8},{8,16},{16,24},{24,1},{1,9},{9,17},{17,25},{25,2},{2,10},{10... | collective-permute-start | bytes 884744 | tf_op jit(solution)/shard_map/ppermute | solution.py:52
  92.3 3.5 %collective-permute-start.11 = (f32[6,3,32,128]{3,2,1,0:T(8,128)S(1)}, f32[6,3,32,128]{3,2,1,0:T(8,128)S(1)}, u32[]{:S(2)}, u32[]{:S(2)}) collective-permute-start(f32[6,3,32,128]{3,2,1,0:T(8,128)S(1)} %get-tuple-element.50), channel_id=1, source_target_pairs={{8,0},{16,8},{24,16},{1,24},{9,1},{17,9},{25,17},{2,25},{10,2},{18... | collective-permute-start | bytes 884744 | tf_op jit(solution)/shard_map/ppermute | solution.py:53
  99.9 8.7 %collective-permute-start.12 = (f32[6,3,32,128]{3,2,1,0:T(8,128)S(1)}, f32[6,3,32,128]{3,2,1,0:T(8,128)S(1)}, u32[]{:S(2)}, u32[]{:S(2)}) collective-permute-start(f32[6,3,32,128]{3,2,1,0:T(8,128)S(1)} %get-tuple-element.49), channel_id=1, source_target_pairs={{0,8},{8,16},{16,24},{24,1},{1,9},{9,17},{17,25},{25,2},{2,10},{10... | collective-permute-start | bytes 884744 | tf_op jit(solution)/shard_map/ppermute | solution.py:52
  107.3 3.5 %collective-permute-start.13 = (f32[6,3,32,128]{3,2,1,0:T(8,128)S(1)}, f32[6,3,32,128]{3,2,1,0:T(8,128)S(1)}, u32[]{:S(2)}, u32[]{:S(2)}) collective-permute-start(f32[6,3,32,128]{3,2,1,0:T(8,128)S(1)} %get-tuple-element.48), channel_id=1, source_target_pairs={{8,0},{16,8},{24,16},{1,24},{9,1},{17,9},{25,17},{2,25},{10,2},{18... | collective-permute-start | bytes 884744 | tf_op jit(solution)/shard_map/ppermute | solution.py:53
  114.9 8.7 %collective-permute-start.14 = (f32[6,3,32,128]{3,2,1,0:T(8,128)S(1)}, f32[6,3,32,128]{3,2,1,0:T(8,128)S(1)}, u32[]{:S(2)}, u32[]{:S(2)}) collective-permute-start(f32[6,3,32,128]{3,2,1,0:T(8,128)S(1)} %get-tuple-element.47), channel_id=1, source_target_pairs={{0,8},{8,16},{16,24},{24,1},{1,9},{9,17},{17,25},{25,2},{2,10},{10... | collective-permute-start | bytes 884744 | tf_op jit(solution)/shard_map/ppermute | solution.py:52
  122.3 3.5 %collective-permute-start.15 = (f32[6,3,32,128]{3,2,1,0:T(8,128)S(1)}, f32[6,3,32,128]{3,2,1,0:T(8,128)S(1)}, u32[]{:S(2)}, u32[]{:S(2)}) collective-permute-start(f32[6,3,32,128]{3,2,1,0:T(8,128)S(1)} %get-tuple-element.46), channel_id=1, source_target_pairs={{8,0},{16,8},{24,16},{1,24},{9,1},{17,9},{25,17},{2,25},{10,2},{18... | collective-permute-start | bytes 884744 | tf_op jit(solution)/shard_map/ppermute | solution.py:53
  129.9 8.7 %collective-permute-start.16 = (f32[3,3,32,128]{3,2,1,0:T(8,128)S(1)}, f32[3,3,32,128]{3,2,1,0:T(8,128)S(1)}, u32[]{:S(2)}, u32[]{:S(2)}) collective-permute-start(f32[3,3,32,128]{3,2,1,0:T(8,128)S(1)} %get-tuple-element.45), channel_id=1, source_target_pairs={{0,8},{8,16},{16,24},{24,1},{1,9},{9,17},{17,25},{25,2},{2,10},{10... | collective-permute-start | bytes 442376 | tf_op jit(solution)/shard_map/ppermute | solution.py:52
  137.3 3.3 %collective-permute-start.17 = (f32[3,3,32,128]{3,2,1,0:T(8,128)S(1)}, f32[3,3,32,128]{3,2,1,0:T(8,128)S(1)}, u32[]{:S(2)}, u32[]{:S(2)}) collective-permute-start(f32[3,3,32,128]{3,2,1,0:T(8,128)S(1)} %get-tuple-element.44), channel_id=1, source_target_pairs={{8,0},{16,8},{24,16},{1,24},{9,1},{17,9},{25,17},{2,25},{10,2},{18... | collective-permute-start | bytes 442376 | tf_op jit(solution)/shard_map/ppermute | solution.py:53
  142.9 5.9 %collective-permute-start.18 = (f32[1,128]{1,0:T(1,128)S(1)}, f32[1,128]{1,0:T(1,128)S(1)}, u32[]{:S(2)}, u32[]{:S(2)}) collective-permute-start(f32[1,128]{1,0:T(1,128)S(1)} %pad_bitcast_fusion), channel_id=1, source_target_pairs={{0,8},{8,0},{16,24},{24,16},{1,9},{9,1},{17,25},{25,17},{2,10},{10... | collective-permute-start | bytes 1544 | tf_op jit(solution)/shard_map/ppermute | solution.py:361
  148.8 5.0 %collective-permute-start.19 = (f32[1,128]{1,0:T(1,128)S(1)}, f32[1,128]{1,0:T(1,128)S(1)}, u32[]{:S(2)}, u32[]{:S(2)}) collective-permute-start(f32[1,128]{1,0:T(1,128)S(1)} %fusion), channel_id=1, source_target_pairs={{0,16},{8,24},{16,0},{24,8},{1,17},{9,25},{17,1},{25,9},{2,18},{10... | collective-permute-start | bytes 1544 | tf_op jit(solution)/shard_map/ppermute | solution.py:361
  153.7 6.9 %collective-permute-start.20 = (f32[1,128]{1,0:T(1,128)S(1)}, f32[1,128]{1,0:T(1,128)S(1)}, u32[]{:S(2)}, u32[]{:S(2)}) collective-permute-start(f32[1,128]{1,0:T(1,128)S(1)} %add.22), channel_id=1, source_target_pairs={{0,1},{1,0},{2,3},{3,2},{4,5},{5,4},{6,7},{7,6},{8,9},{9,8},{10,11... | collective-permute-start | bytes 1544 | tf_op jit(solution)/shard_map/ppermute | solution.py:361
  160.7 3.6 %collective-permute-start.21 = (f32[1,128]{1,0:T(1,128)S(1)}, f32[1,128]{1,0:T(1,128)S(1)}, u32[]{:S(2)}, u32[]{:S(2)}) collective-permute-start(f32[1,128]{1,0:T(1,128)S(1)} %add.23), channel_id=1, source_target_pairs={{0,2},{1,3},{2,0},{3,1},{4,6},{5,7},{6,4},{7,5},{8,10},{9,11},{10,... | collective-permute-start | bytes 1544 | tf_op jit(solution)/shard_map/ppermute | solution.py:361
  164.3 4.5 %collective-permute-start.22 = (f32[1,128]{1,0:T(1,128)S(1)}, f32[1,128]{1,0:T(1,128)S(1)}, u32[]{:S(2)}, u32[]{:S(2)}) collective-permute-start(f32[1,128]{1,0:T(1,128)S(1)} %add.24), channel_id=1, source_target_pairs={{0,4},{1,5},{2,6},{3,7},{4,0},{5,1},{6,2},{7,3},{8,12},{9,13},{10,... | collective-permute-start | bytes 1544 | tf_op jit(solution)/shard_map/ppermute | solution.py:361
